TPU v7x, 32 devices: a whole 2x2x4 slice. The times are simulated.
32 devices in a mesh: dev: 32 (over z, y, x, core).
Axes of the slice: x: 2, y: 2, z: 4, core: 2. Of those that a mesh axis runs over, the one named last changes fastest.
Arguments:
- embeddings: float32 [8192, 1024], P('dev'), may hold values from -6 to 6
- lists: int32 [8192], P('dev'), may hold values from 0 to 65535, as said below
- row_ids: int32 [8192], P('dev'), may hold values from 0 to 8191, each once
- centroids: float32 [65536, 1024], P('dev'), may hold values from -6 to 6
- rotation: float32 [1024, 1024], replicated, may hold values from -0.1875 to 0.1875
Outputs:
- packed: float32 [16384, 1024], P('dev')
- packed_ids: int32 [16384], P('dev')
- list_offsets: int32 [65536], P('dev')
Inputs may be any that keep to these rules, and one draw needn't show every extreme that they name: Lists l * 2048 to (l + 1) * 2048 - 1 belong to owner l. Among the rows of one device, at most 16 have lists of one owner, so an owner receives at most 512 rows; in every draw some owner receives exactly 16 rows from every device. `row_ids`: all identifiers are distinct.
All inputs are finite; a program needn't handle non-finite values.
Results may differ from a plain program's by a relative error of at most 0.0003.
Values sent between devices are 32-bit elements; how exact they have to be, the bound alone decides.
A program may use at most 64 MiB of HBM per device.

v0:
```python
import functools

import jax
import jax.numpy as jnp
from jax import lax
from jax.experimental import pallas as pl
from jax.experimental.pallas import tpu as pltpu
from jax.sharding import PartitionSpec as P

MESH = pl.DeviceIdType.MESH
F32 = jnp.float32
BF16 = jnp.bfloat16
LANES = 128


def split(x):
    hi = x.astype(BF16)
    lo = (x - hi.astype(F32)).astype(BF16)
    return hi, lo


def dot(a, b):
    return jnp.dot(a, b, preferred_element_type=F32)


def kernel(
    n, slots, chunks,
    send, meta, cent, rot,
    out, ids_out, off_out,
    recv, meta_in, cent_buf, rot_buf, rot_hi, rot_lo, res, place,
    send_sem, recv_sem, meta_send_sem, meta_recv_sem, own_sem, load_sem,
):
    me = lax.axis_index("dev")
    cap, width = out.shape
    owned = cent.shape[0]
    entries = n * slots
    groups = entries // LANES
    per = LANES // slots
    wide = width // chunks

    load_cent = pltpu.make_async_copy(cent, cent_buf, load_sem.at[0])
    load_rot = pltpu.make_async_copy(rot, rot_buf, load_sem.at[1])
    own_meta = pltpu.make_async_copy(meta.at[me], meta_in.at[me], own_sem.at[chunks])

    def own_rows(c):
        cols = pl.ds(pl.multiple_of(c * wide, wide), wide)
        return pltpu.make_async_copy(send.at[me, :, cols], recv.at[c, me], own_sem.at[c])

    barrier = pltpu.get_barrier_semaphore()

    def greet(k, carry):
        peer = lax.rem(me + k, n)
        pl.semaphore_signal(barrier, inc=1, device_id=(peer,), device_id_type=MESH)
        return carry

    lax.fori_loop(1, n, greet, 0)
    own_meta.start()
    pl.semaphore_wait(barrier, n - 1)

    def peer_of(j):
        k = n // 2 + (2 * lax.rem(j, 2) - 1) * lax.div(j + 1, 2)
        return lax.rem(me + k, n)

    def send_meta(j, carry):
        peer = peer_of(j)
        pltpu.make_async_remote_copy(
            src_ref=meta.at[peer], dst_ref=meta_in.at[me],
            send_sem=meta_send_sem, recv_sem=meta_recv_sem,
            device_id=(peer,), device_id_type=MESH,
        ).start()
        return carry

    lax.fori_loop(0, n - 1, send_meta, 0)

    for c in range(chunks):
        def send_rows(j, carry):
            peer = peer_of(j)
            pltpu.make_async_remote_copy(
                src_ref=send.at[peer, :, pl.ds(c * wide, wide)], dst_ref=recv.at[c, me],
                send_sem=send_sem.at[c], recv_sem=recv_sem.at[c],
                device_id=(peer,), device_id_type=MESH,
            ).start()
            return carry

        lax.fori_loop(0, n - 1, send_rows, 0)

    load_cent.start()
    load_rot.start()
    for c in range(chunks):
        own_rows(c).start()

    most = pl.ds(0, n - 1)
    pltpu.make_async_copy(meta_in.at[most], meta_in.at[most], meta_recv_sem).wait()
    own_meta.wait()

    list_row, id_row, key_row, key_col, list_col, id_col = [], [], [], [], [], []
    lane = lax.broadcasted_iota(jnp.int32, (1, LANES), 1)
    for g in range(groups):
        got = jnp.sum(meta_in[pl.ds(g * per, per)], axis=0)
        found = got[0:1] - 1
        safe = jnp.where(found >= 0, found, owned)
        key = safe * entries + (g * LANES) + lane
        list_row.append(safe)
        id_row.append(got[1:2])
        key_row.append(key)
        key_col.append(jnp.transpose(jnp.broadcast_to(key, (LANES, LANES))))
        list_col.append(jnp.transpose(jnp.broadcast_to(safe, (LANES, LANES))))
        id_col.append(jnp.transpose(jnp.broadcast_to(got[1:2], (LANES, LANES))))

    slot_at = lax.broadcasted_iota(jnp.int32, (cap, LANES), 0)
    slot_list = jnp.zeros((cap, LANES), jnp.int32)
    pos_col = []
    for g in range(groups):
        rank = jnp.zeros((1, LANES), jnp.int32)
        for h in range(groups):
            less = (key_col[h] < key_row[g]).astype(jnp.int32)
            rank = rank + jnp.sum(less, axis=0, keepdims=True)
        rank = jnp.where(list_row[g] < owned, rank, cap + entries)
        hit = slot_at == rank
        place[:, pl.ds(g * LANES, LANES)] = hit.astype(F32).astype(BF16)
        slot_list = slot_list + jnp.where(hit, list_row[g] + 1, 0)
        pos_col.append(jnp.transpose(jnp.broadcast_to(rank, (LANES, LANES))))
    at_list = jnp.sum(slot_list, axis=1, keepdims=True) - 1

    for q in range(cap // LANES):
        total = jnp.zeros((1, LANES), jnp.int32)
        for g in range(groups):
            hit = pos_col[g] == lane + q * LANES
            total = total + jnp.sum(jnp.where(hit, id_col[g] + 1, 0), axis=0, keepdims=True)
        ids_out[pl.ds(q, 1), :] = total - 1
    for q in range(owned // LANES):
        total = jnp.zeros((1, LANES), jnp.int32)
        for g in range(groups):
            less = (list_col[g] < lane + q * LANES).astype(jnp.int32)
            total = total + jnp.sum(less, axis=0, keepdims=True)
        off_out[pl.ds(q, 1), :] = total

    res[...] = jnp.zeros_like(res)
    load_cent.wait()
    step = 256

    def centre(t, carry):
        base = pl.multiple_of(t * step, step)
        table = lax.broadcasted_iota(jnp.int32, (cap, step), 1) + base
        pick = (table == at_list).astype(F32).astype(BF16)
        for c in range(chunks):
            cols = pl.ds(c * wide, wide)
            hi, lo = split(cent_buf[pl.ds(base, step), cols])
            res[:, cols] -= dot(pick, hi) + dot(pick, lo)
        return carry

    lax.fori_loop(0, owned // step, centre, 0)

    load_rot.wait()

    def halve(t, carry):
        rows = pl.ds(pl.multiple_of(t * LANES, LANES), LANES)
        hi, lo = split(rot_buf[rows, :])
        rot_hi[rows, :] = hi
        rot_lo[rows, :] = lo
        return carry

    lax.fori_loop(0, width // LANES, halve, 0)
    out[...] = jnp.zeros_like(out)

    def turn(c, carry):
        pltpu.make_async_copy(recv.at[c, most], recv.at[c, most], recv_sem.at[c]).wait()
        own_rows(c).wait()
        cols = pl.ds(pl.multiple_of(c * wide, wide), wide)
        hi, lo = split(recv[c].reshape(entries, wide))
        spots = place[...]
        left = res[:, cols] + (dot(spots, hi) + dot(spots, lo))
        left_hi, left_lo = split(left)

        def tile(t, inner):
            at = pl.ds(pl.multiple_of(t * 256, 256), 256)
            r_hi = rot_hi[cols, at]
            r_lo = rot_lo[cols, at]
            out[:, at] += dot(left_hi, r_hi) + dot(left_lo, r_hi) + dot(left_hi, r_lo)
            return inner

        lax.fori_loop(0, width // 256, tile, 0)
        return carry

    lax.fori_loop(0, chunks, turn, 0)

    pltpu.make_async_copy(meta_in.at[most], meta_in.at[most], meta_send_sem).wait()
    for c in range(chunks):
        pltpu.make_async_copy(recv.at[c, most], recv.at[c, most], send_sem.at[c]).wait()


def full(embeddings, lists, row_ids, centroids, rotation):
    rows, width = embeddings.shape
    owned = centroids.shape[0]
    n = lax.axis_size("dev")
    cap = 2 * rows
    slots = max(8, cap // n)
    chunks = 4
    entries = n * slots
    me = lax.axis_index("dev")
    owner = lists // owned
    index = jnp.arange(rows, dtype=jnp.int32)
    earlier = index[None, :] < index[:, None]
    slot = jnp.sum((owner[None, :] == owner[:, None]) & earlier, axis=1).astype(jnp.int32)
    target = owner * slots + slot
    table = jnp.arange(entries, dtype=jnp.int32)
    match = target[None, :] == table[:, None]
    send = jnp.dot(match.astype(F32), embeddings, precision=lax.Precision.HIGH, preferred_element_type=F32)
    send = send.reshape(n, slots, width)
    per = LANES // slots
    own_lanes = (jnp.arange(LANES, dtype=jnp.int32) // slots) == lax.rem(me, per)

    def spread(values):
        picked = jnp.sum(jnp.where(match, values[None, :], 0), axis=1).astype(jnp.int32)
        return jnp.where(own_lanes[None, :], jnp.tile(picked.reshape(n, slots), (1, per)), 0)

    meta = jnp.zeros((n, 8, LANES), jnp.int32)
    meta = jnp.stack([spread(lists - owner * owned + 1), spread(row_ids)] + [jnp.zeros((n, LANES), jnp.int32)] * 6, axis=1)
    wide = width // chunks
    vmem = pl.BlockSpec(memory_space=pltpu.VMEM)
    hbm = pl.BlockSpec(memory_space=pltpu.HBM)
    packed, ids, offsets = pl.pallas_call(
        functools.partial(kernel, n, slots, chunks),
        out_shape=(
            jax.ShapeDtypeStruct((cap, width), F32),
            jax.ShapeDtypeStruct((cap // LANES, LANES), jnp.int32),
            jax.ShapeDtypeStruct((owned // LANES, LANES), jnp.int32),
        ),
        in_specs=[hbm, hbm, hbm, hbm],
        out_specs=(vmem, vmem, vmem),
        scratch_shapes=[
            pltpu.VMEM((chunks, n, slots, wide), F32),
            pltpu.VMEM((n, 8, LANES), jnp.int32),
            pltpu.VMEM((owned, width), F32),
            pltpu.VMEM((width, width), F32),
            pltpu.VMEM((width, width), BF16),
            pltpu.VMEM((width, width), BF16),
            pltpu.VMEM((cap, width), F32),
            pltpu.VMEM((cap, entries), BF16),
            pltpu.SemaphoreType.DMA((chunks,)),
            pltpu.SemaphoreType.DMA((chunks,)),
            pltpu.SemaphoreType.DMA,
            pltpu.SemaphoreType.DMA,
            pltpu.SemaphoreType.DMA((chunks + 1,)),
            pltpu.SemaphoreType.DMA((2,)),
        ],
        compiler_params=pltpu.CompilerParams(
            collective_id=1, has_side_effects=True, vmem_limit_bytes=48 * 1024 * 1024
        ),
    )(send, meta, centroids, rotation)
    return packed


def pack(n, slots, ka, kb, pool, owned, emb, lists, ids, a_out, b_out, x_out, meta_out):
    me = lax.axis_index("dev")
    count, width = emb.shape
    tall = width // LANES
    parts = count // LANES
    per = LANES // slots
    lane = lax.broadcasted_iota(jnp.int32, (1, LANES), 1)
    lanes = lax.broadcasted_iota(jnp.int32, (LANES, LANES), 1)
    ahead = lax.broadcasted_iota(jnp.int32, (LANES, LANES), 0) < lanes

    def column_of(row):
        return jnp.transpose(jnp.broadcast_to(row, (LANES, LANES)))

    def hot(mask):
        return mask.astype(F32).astype(BF16)

    list_row = [lists[r:r + 1, :] for r in range(parts)]
    id_row = [ids[r:r + 1, :] for r in range(parts)]
    owner_row = [lax.div(x, owned) for x in list_row]
    owner_col = [column_of(x) for x in owner_row]
    slot_row, past_row, past_col = [], [], []
    for r in range(parts):
        slot = jnp.zeros((1, LANES), jnp.int32)
        for q in range(r + 1):
            same = owner_col[q] == owner_row[r]
            if q == r:
                same = same & ahead
            slot = slot + jnp.sum(same.astype(jnp.int32), axis=0, keepdims=True)
        past = (slot >= ka + kb).astype(jnp.int32)
        slot_row.append(slot)
        past_row.append(past)
        past_col.append(column_of(past))
    total = jnp.zeros((1, LANES), jnp.int32)
    spill_row = []
    for r in range(parts):
        here = jnp.sum(jnp.where(ahead, past_col[r], 0), axis=0, keepdims=True)
        spill_row.append(total + here)
        total = total + jnp.sum(past_col[r], axis=0, keepdims=True)
    wanted = n * (ka + kb) + pool
    table = lax.broadcasted_iota(jnp.int32, (wanted, LANES), 0)
    picks = []
    for r in range(parts):
        owner, slot, past = owner_row[r], slot_row[r], past_row[r]
        target = jnp.where(
            slot < ka, owner * ka + slot,
            jnp.where(past > 0, n * (ka + kb) + spill_row[r], n * ka + owner * kb + slot - ka),
        )
        picks.append(hot(table == target))
    pick = jnp.concatenate(picks, axis=1)
    for b in range(0, tall, 2):
        hi, lo = split(emb[:, b * LANES:(b + 2) * LANES])
        value = dot(pick, hi) + dot(pick, lo)
        for h in range(2):
            got = value[:, h * LANES:(h + 1) * LANES]
            a_out[pl.ds(b + h, n * ka, stride=tall), :] = got[:n * ka]
            b_out[pl.ds(b + h, n * kb, stride=tall), :] = got[n * ka:n * (ka + kb)]
            x_out[pl.ds(b + h, pool, stride=tall), :] = got[n * (ka + kb):]

    base = lax.rem(me, per) * slots
    owners = lax.broadcasted_iota(jnp.int32, (n, LANES), 0)
    spots = [hot(column_of(slot_row[r]) + base == lanes) for r in range(parts)]
    local_row = [list_row[r] - owner_row[r] * owned + 1 for r in range(parts)]
    held_row = [
        jnp.where((past_row[r] > 0) & (spill_row[r] < pool), spill_row[r] + 1, 0) for r in range(parts)
    ]
    for at, values in enumerate((local_row, id_row, held_row)):
        high = jnp.zeros((n, LANES), F32)
        low = jnp.zeros((n, LANES), F32)
        for r in range(parts):
            mine = owners == owner_row[r]
            upper = lax.div(values[r], 256)
            lower = values[r] - upper * 256
            high = high + dot(jnp.where(mine, upper, 0).astype(F32).astype(BF16), spots[r])
            low = low + dot(jnp.where(mine, lower, 0).astype(F32).astype(BF16), spots[r])
        meta_out[:, at, :] = high.astype(jnp.int32) * 256 + low.astype(jnp.int32)
    meta_out[:, 3, :] = jnp.broadcast_to(total, (n, LANES))


def pooled_kernel(
    n, slots, ka, kb, pool, deep,
    emb, lists, ids, cent, rot,
    out, ids_out, off_out, most_out,
    send_a, send_b, extra, meta, in_a, in_b, in_x, meta_in, cent_buf, rot_buf, rot_hi, rot_lo, res,
    send_sem, recv_sem, load_sem,
):
    me = lax.axis_index("dev")
    cap, width = out.shape
    owned = cent.shape[0]
    entries = n * slots
    groups = entries // LANES
    per = LANES // slots
    tall = width // LANES
    flat = n // (2 * deep)
    META, A, B, X1, X2, X3 = range(6)

    def rows(index, count):
        return pl.ds(pl.multiple_of(index * (count * tall), 8), count * tall)

    load_cent = pltpu.make_async_copy(cent, cent_buf, load_sem.at[0])
    load_rot = pltpu.make_async_copy(rot, rot_buf, load_sem.at[1])
    core = lax.rem(me, 2)
    column = lax.rem(lax.div(me, 2), flat)
    level = lax.div(me, 2 * flat)
    spot = (core * flat + column) * deep + level

    barrier = pltpu.get_barrier_semaphore()

    def greet(k, carry):
        peer = lax.rem(me + k, n)
        pl.semaphore_signal(barrier, inc=1, device_id=(peer,), device_id_type=MESH)
        return carry

    lax.fori_loop(1, n, greet, 0)
    load_cent.start()
    load_rot.start()
    pack(n, slots, ka, kb, pool, owned, emb, lists, ids, send_a, send_b, extra, meta)
    meta_in[pl.ds(me, 1)] = meta[pl.ds(me, 1)]
    in_a[rows(me, ka), :] = send_a[rows(me, ka), :]
    in_b[rows(me, kb), :] = send_b[rows(me, kb), :]
    in_x[rows(spot, pool), :] = extra[...]
    pl.semaphore_wait(barrier, n - 1)

    def post(src, dst, peer, at):
        pltpu.make_async_remote_copy(
            src_ref=src, dst_ref=dst, send_sem=send_sem.at[at], recv_sem=recv_sem.at[at],
            device_id=(peer,), device_id_type=MESH,
        ).start()

    def peer_of(j):
        k = n // 2 + (2 * lax.rem(j, 2) - 1) * lax.div(j + 1, 2)
        return lax.rem(me + k, n)

    def send_meta(j, carry):
        peer = peer_of(j)
        post(meta.at[peer], meta_in.at[me], peer, META)
        return carry

    def send_level(k, carry):
        peer = lax.rem(level + k, deep) * (2 * flat) + column * 2 + core
        post(extra, in_x.at[rows(spot, pool)], peer, X1)
        return carry

    def send_column(k, carry):
        peer = level * (2 * flat) + lax.rem(column + k, flat) * 2 + core
        block = in_x.at[rows(core * flat + column, deep * pool)]
        post(block, block, peer, X2)
        return carry

    def send_a_rows(j, carry):
        peer = peer_of(j)
        post(send_a.at[rows(peer, ka)], in_a.at[rows(me, ka)], peer, A)
        return carry

    def send_b_rows(j, carry):
        peer = peer_of(j)
        post(send_b.at[rows(peer, kb)], in_b.at[rows(me, kb)], peer, B)
        return carry

    def settle(ref, sem):
        pltpu.make_async_copy(ref, ref, sem).wait()

    span_meta = meta_in.at[pl.ds(0, n - 1)]
    span_a = in_a.at[pl.ds(0, (n - 1) * ka * tall)]
    span_b = in_b.at[pl.ds(0, (n - 1) * kb * tall)]
    span_1 = in_x.at[pl.ds(0, (deep - 1) * pool * tall)]
    span_2 = in_x.at[pl.ds(0, (flat - 1) * deep * pool * tall)]
    span_3 = in_x.at[pl.ds(0, flat * deep * pool * tall)]

    lax.fori_loop(0, n - 1, send_meta, 0)
    lax.fori_loop(1, deep, send_level, 0)
    lax.fori_loop(0, n - 1, send_a_rows, 0)

    settle(span_meta, recv_sem.at[META])

    list_row, key_row, key_col, list_col, id_col, pool_col = [], [], [], [], [], []
    lane = lax.broadcasted_iota(jnp.int32, (1, LANES), 1)
    most = jnp.zeros((1, LANES), jnp.int32)

    def column_of(row):
        return jnp.transpose(jnp.broadcast_to(row, (LANES, LANES)))

    for g in range(groups):
        block = meta_in[pl.ds(g * per, per)]
        got = jnp.sum(block, axis=0)
        most = jnp.maximum(most, jnp.max(block, axis=0)[3:4])
        found = got[0:1] - 1
        safe = jnp.where(found >= 0, found, owned)
        entry = g * LANES + lane
        key = safe * entries + entry
        source = entry // slots
        place_of = (lax.rem(source, 2) * flat + lax.rem(source // 2, flat)) * deep + source // (2 * flat)
        spill = jnp.where(got[2:3] > 0, place_of * pool + got[2:3] - 1, n * pool)
        list_row.append(safe)
        key_row.append(key)
        key_col.append(column_of(key))
        list_col.append(column_of(safe))
        id_col.append(column_of(got[1:2]))
        pool_col.append(column_of(spill))
    most_out[...] = most

    slot_at = lax.broadcasted_iota(jnp.int32, (cap, LANES), 0)
    slot_list = jnp.zeros((cap, LANES), jnp.int32)
    pos_col = []
    hits = []
    for g in range(groups):
        rank = jnp.zeros((1, LANES), jnp.int32)
        for h in range(groups):
            less = (key_col[h] < key_row[g]).astype(jnp.int32)
            rank = rank + jnp.sum(less, axis=0, keepdims=True)
        rank = jnp.where(list_row[g] < owned, rank, cap + entries)
        hit = slot_at == rank
        hits.append(hit.astype(F32).astype(BF16))
        slot_list = slot_list + jnp.where(hit, list_row[g] + 1, 0)
        pos_col.append(column_of(rank))
    at_list = jnp.sum(slot_list, axis=1, keepdims=True) - 1

    def onto(count, columns_of):
        total = jnp.zeros((cap, count), F32)
        at = lax.broadcasted_iota(jnp.int32, (LANES, count), 1)
        for g in range(groups):
            wanted = jnp.broadcast_to(columns_of(g)[:, 0:1], (LANES, count))
            total = total + dot(hits[g], (wanted == at).astype(F32).astype(BF16))
        return total.astype(BF16)

    def direct(first, count):
        def columns_of(g):
            entry = g * LANES + lax.broadcasted_iota(jnp.int32, (LANES, LANES), 0)
            inside = lax.rem(entry, slots) - first
            return jnp.where((inside >= 0) & (inside < count), (entry // slots) * count + inside, -1)
        return columns_of

    place_a = onto(n * ka, direct(0, ka))
    place_b = onto(n * kb, direct(ka, kb))
    place_x = onto(n * pool, lambda g: pool_col[g])

    settle(span_1, recv_sem.at[X1])
    lax.fori_loop(1, flat, send_column, 0)
    lax.fori_loop(0, n - 1, send_b_rows, 0)

    for q in range(cap // LANES):
        total = jnp.zeros((1, LANES), jnp.int32)
        for g in range(groups):
            hit = pos_col[g] == lane + q * LANES
            total = total + jnp.sum(jnp.where(hit, id_col[g] + 1, 0), axis=0, keepdims=True)
        ids_out[pl.ds(q, 1), :] = total - 1
    for q in range(owned // LANES):
        total = jnp.zeros((1, LANES), jnp.int32)
        for g in range(groups):
            less = (list_col[g] < lane + q * LANES).astype(jnp.int32)
            total = total + jnp.sum(less, axis=0, keepdims=True)
        off_out[pl.ds(q, 1), :] = total

    res[...] = jnp.zeros_like(res)
    load_cent.wait()
    step = 256

    def centre(t, carry):
        base = pl.multiple_of(t * step, step)
        table = lax.broadcasted_iota(jnp.int32, (cap, step), 1) + base
        pick = (table == at_list).astype(F32).astype(BF16)
        for c in range(width // step):
            cols = pl.ds(c * step, step)
            hi, lo = split(cent_buf[pl.ds(base, step), cols])
            res[:, cols] -= dot(pick, hi) + dot(pick, lo)
        return carry

    lax.fori_loop(0, owned // step, centre, 0)

    settle(span_2, recv_sem.at[X2])
    half = in_x.at[rows(core, flat * deep * pool)]
    post(half, half, me + 1 - 2 * core, X3)

    load_rot.wait()

    def halve(t, carry):
        at = pl.ds(pl.multiple_of(t * LANES, LANES), LANES)
        hi, lo = split(rot_buf[at, :])
        rot_hi[at, :] = hi
        rot_lo[at, :] = lo
        return carry

    lax.fori_loop(0, width // LANES, halve, 0)

    def piece(ref, count, b):
        return ref[pl.ds(b, count, stride=tall), :]

    settle(span_3, recv_sem.at[X3])
    for b in range(0, tall, 2):
        cols = pl.ds(b * LANES, 2 * LANES)
        hi, lo = split(jnp.concatenate([piece(in_x, n * pool, b), piece(in_x, n * pool, b + 1)], axis=1))
        res[:, cols] += dot(place_x, hi) + dot(place_x, lo)

    settle(span_a, recv_sem.at[A])
    for b in range(0, tall, 2):
        cols = pl.ds(b * LANES, 2 * LANES)
        hi, lo = split(jnp.concatenate([piece(in_a, n * ka, b), piece(in_a, n * ka, b + 1)], axis=1))
        left_hi, left_lo = split(res[:, cols] + dot(place_a, hi) + dot(place_a, lo))

        def tile(t, carry):
            at = pl.ds(pl.multiple_of(t * 256, 256), 256)
            r_hi = rot_hi[cols, at]
            r_lo = rot_lo[cols, at]
            value = dot(left_hi, r_hi) + dot(left_lo, r_hi) + dot(left_hi, r_lo)
            if b == 0:
                out[:, at] = value
            else:
                out[:, at] += value
            return carry

        lax.fori_loop(0, width // 256, tile, 0)

    settle(span_b, recv_sem.at[B])
    last_hi, last_lo = split(jnp.concatenate([piece(in_b, n * kb, b) for b in range(tall)], axis=1))

    def finish(t, carry):
        at = pl.ds(pl.multiple_of(t * 256, 256), 256)
        r_hi = rot_hi[:, at]
        r_lo = rot_lo[:, at]
        hi, lo = split(dot(last_hi, r_hi) + dot(last_lo, r_hi) + dot(last_hi, r_lo))
        out[:, at] += dot(place_b, hi) + dot(place_b, lo)
        return carry

    lax.fori_loop(0, width // 256, finish, 0)

    settle(span_meta, send_sem.at[META])
    settle(span_a, send_sem.at[A])
    settle(span_b, send_sem.at[B])
    settle(span_1, send_sem.at[X1])
    settle(span_2, send_sem.at[X2])
    settle(span_3, send_sem.at[X3])


def local(embeddings, lists, row_ids, centroids, rotation):
    row_count, width = embeddings.shape
    owned = centroids.shape[0]
    n = lax.axis_size("dev")
    cap = 2 * row_count
    real = cap // n
    slots = max(8, real)
    ka, kb = (7 * real + 15) // 16, real // 4
    pool = 12
    deep = 2
    while deep * deep * 8 <= n:
        deep *= 2
    tall = width // LANES
    by_lane = (row_count // LANES, LANES)
    vmem = pl.BlockSpec(memory_space=pltpu.VMEM)
    hbm = pl.BlockSpec(memory_space=pltpu.HBM)
    packed, ids, offsets, most = pl.pallas_call(
        functools.partial(pooled_kernel, n, slots, ka, kb, pool, deep),
        out_shape=(
            jax.ShapeDtypeStruct((cap, width), F32),
            jax.ShapeDtypeStruct((cap // LANES, LANES), jnp.int32),
            jax.ShapeDtypeStruct((owned // LANES, LANES), jnp.int32),
            jax.ShapeDtypeStruct((1, LANES), jnp.int32),
        ),
        in_specs=[vmem] * 3 + [hbm] * 2,
        out_specs=(vmem,) * 4,
        scratch_shapes=[
            pltpu.VMEM((n * ka * tall, LANES), F32),
            pltpu.VMEM((n * kb * tall, LANES), F32),
            pltpu.VMEM((pool * tall, LANES), F32),
            pltpu.VMEM((n, 4, LANES), jnp.int32),
            pltpu.VMEM((n * ka * tall, LANES), F32),
            pltpu.VMEM((n * kb * tall, LANES), F32),
            pltpu.VMEM((n * pool * tall, LANES), F32),
            pltpu.VMEM((n, 4, LANES), jnp.int32),
            pltpu.VMEM((owned, width), F32),
            pltpu.VMEM((width, width), F32),
            pltpu.VMEM((width, width), BF16),
            pltpu.VMEM((width, width), BF16),
            pltpu.VMEM((cap, width), F32),
            pltpu.SemaphoreType.DMA((6,)),
            pltpu.SemaphoreType.DMA((6,)),
            pltpu.SemaphoreType.DMA((2,)),
        ],
        compiler_params=pltpu.CompilerParams(
            collective_id=0, has_side_effects=True, vmem_limit_bytes=48 * 1024 * 1024
        ),
    )(embeddings, lists.reshape(by_lane), row_ids.reshape(by_lane), centroids, rotation)
    packed = lax.cond(
        most[0, 0] > pool,
        lambda: full(embeddings, lists, row_ids, centroids, rotation),
        lambda: packed,
    )
    packed = jnp.where(ids.reshape(-1)[:, None] >= 0, packed, 0.0)
    return packed, ids.reshape(-1), offsets.reshape(-1)


def solution(mesh):
    in_specs = (P("dev", None), P("dev"), P("dev"), P("dev", None), P())
    out_specs = (P("dev", None), P("dev"), P("dev"))
    return jax.shard_map(local, mesh=mesh, in_specs=in_specs, out_specs=out_specs, check_vma=False)
```

profile of v0, /device:TPU:0, one launch (start us, length us, event | category | flops | bytes accessed | tf_op | source)
XLA Modules:
  0.0 55.0 jit_solution(10004186939518144782)
XLA Ops:
  0.6 0.0 copy-start
  0.6 0.0 copy-start.1
  0.7 0.0 copy-start.2
  0.7 51.3 %shard_map.76 = (f32[512,1024]{1,0:T(8,128)S(1)}, s32[4,128]{1,0:T(4,128)S(1)}, s32[16,128]{1,0:T(8,128)S(1)}, s32[1,128]{1,0:T(1,128)S(1)}) custom-call(f32[256,1024]{1,0:T(8,128)} %emb.1, s32[2,128]{1,0:T(2,128)} %bitcast.17, s32[2,128]{1,0:T(2,128)} %bitcast.18, f32[2048,1024]{1,0:T(8,128)} %cent.1, f32[1024,1024]{1,0:T(8,128)} %rot.1), custom_call_target="tpu_custom_call" | custom-call | tf_op jit(solution)/shard_map/pallas_call | solution.py:602
  52.0 0.0 copy-done
  52.1 0.0 copy-done.1
  52.1 0.0 copy-done.2
  52.1 0.2 conditional.1
  52.3 1.5 %broadcast_select_fusion.2 = f32[512,1024]{1,0:T(8,128)} fusion(f32[512,1024]{1,0:T(8,128)S(1)} %get-tuple-element.43, pred[512]{0:T(512)(128)(4,1)S(1)} %broadcast_compare_fusion), kind=kLoop, calls=%fused_computation.22 | loop fusion | flops 524288 | bytes 4194816 | tf_op jit(solution)/shard_map/jit(_where)/select_n | solution.py:639
  53.8 0.6 %copy.20 = s32[512]{0:T(512)} copy(s32[512]{0:T(512)S(1)} %bitcast.12) | data formatting | bytes 4096
  54.4 0.6 %copy.21 = s32[2048]{0:T(1024)} copy(s32[2048]{0:T(1024)S(1)} %bitcast.13) | data formatting | bytes 16384
  (1 shorter events, 0.0 us)
Async XLA Ops:
  0.6 51.4 %copy-start = (f32[256,1024]{1,0:T(8,128)S(1)}, f32[256,1024]{1,0:T(8,128)}, u32[]{:S(2)}) copy-start(f32[256,1024]{1,0:T(8,128)} %emb.1) | copy-start | bytes 3145732
  0.6 51.4 %copy-start.1 = (s32[256]{0:T(256)S(1)}, s32[256]{0:T(256)}, u32[]{:S(2)}) copy-start(s32[256]{0:T(256)} %param.8) | copy-start | bytes 3076
  0.7 51.4 %copy-start.2 = (s32[256]{0:T(256)S(1)}, s32[256]{0:T(256)}, u32[]{:S(2)}) copy-start(s32[256]{0:T(256)} %param.9) | copy-start | bytes 3076
where the time goes:
time: 56 us; the launch traced here: 55 us
  Pallas kernels  51.3 us (92%)
  other arithmetic  1.53 us (3%)
  local copies, waits for them, and re-layouts  1.19 us (2%)
  between operations  0.74 us (1%)
    pallas_call x1, Pallas kernels, local(): pl.pallas_call(functools.partial(pooled_kernel, n, slots, ka, kb, pool, d...  51.3 us
    select_n x1, other arithmetic, local(): packed = jnp.where(ids.reshape(-1)[:, None] >= 0, packed, 0.0)  1.53 us
    unnamed x8, local copies, waits for them, and re-layouts  1.19 us

commit v1 on v0

v1 whole, which is shorter than its diff:
```python
import functools

import jax
import jax.numpy as jnp
from jax import lax
from jax.experimental import pallas as pl
from jax.experimental.pallas import tpu as pltpu
from jax.sharding import PartitionSpec as P

MESH = pl.DeviceIdType.MESH
F32 = jnp.float32
BF16 = jnp.bfloat16
LANES = 128


def split(x):
    hi = x.astype(BF16)
    lo = (x - hi.astype(F32)).astype(BF16)
    return hi, lo


def dot(a, b):
    return jnp.dot(a, b, preferred_element_type=F32)


def kernel(
    n, slots, chunks,
    send, meta, cent, rot,
    out, ids_out, off_out,
    recv, meta_in, cent_buf, rot_buf, rot_hi, rot_lo, res, place,
    send_sem, recv_sem, meta_send_sem, meta_recv_sem, own_sem, load_sem,
):
    me = lax.axis_index("dev")
    cap, width = out.shape
    owned = cent.shape[0]
    entries = n * slots
    groups = entries // LANES
    per = LANES // slots
    wide = width // chunks

    load_cent = pltpu.make_async_copy(cent, cent_buf, load_sem.at[0])
    load_rot = pltpu.make_async_copy(rot, rot_buf, load_sem.at[1])
    own_meta = pltpu.make_async_copy(meta.at[me], meta_in.at[me], own_sem.at[chunks])

    def own_rows(c):
        cols = pl.ds(pl.multiple_of(c * wide, wide), wide)
        return pltpu.make_async_copy(send.at[me, :, cols], recv.at[c, me], own_sem.at[c])

    barrier = pltpu.get_barrier_semaphore()

    def greet(k, carry):
        peer = lax.rem(me + k, n)
        pl.semaphore_signal(barrier, inc=1, device_id=(peer,), device_id_type=MESH)
        return carry

    lax.fori_loop(1, n, greet, 0)
    own_meta.start()
    pl.semaphore_wait(barrier, n - 1)

    def peer_of(j):
        k = n // 2 + (2 * lax.rem(j, 2) - 1) * lax.div(j + 1, 2)
        return lax.rem(me + k, n)

    def send_meta(j, carry):
        peer = peer_of(j)
        pltpu.make_async_remote_copy(
            src_ref=meta.at[peer], dst_ref=meta_in.at[me],
            send_sem=meta_send_sem, recv_sem=meta_recv_sem,
            device_id=(peer,), device_id_type=MESH,
        ).start()
        return carry

    lax.fori_loop(0, n - 1, send_meta, 0)

    for c in range(chunks):
        def send_rows(j, carry):
            peer = peer_of(j)
            pltpu.make_async_remote_copy(
                src_ref=send.at[peer, :, pl.ds(c * wide, wide)], dst_ref=recv.at[c, me],
                send_sem=send_sem.at[c], recv_sem=recv_sem.at[c],
                device_id=(peer,), device_id_type=MESH,
            ).start()
            return carry

        lax.fori_loop(0, n - 1, send_rows, 0)

    load_cent.start()
    load_rot.start()
    for c in range(chunks):
        own_rows(c).start()

    most = pl.ds(0, n - 1)
    pltpu.make_async_copy(meta_in.at[most], meta_in.at[most], meta_recv_sem).wait()
    own_meta.wait()

    list_row, id_row, key_row, key_col, list_col, id_col = [], [], [], [], [], []
    lane = lax.broadcasted_iota(jnp.int32, (1, LANES), 1)
    for g in range(groups):
        got = jnp.sum(meta_in[pl.ds(g * per, per)], axis=0)
        found = got[0:1] - 1
        safe = jnp.where(found >= 0, found, owned)
        key = safe * entries + (g * LANES) + lane
        list_row.append(safe)
        id_row.append(got[1:2])
        key_row.append(key)
        key_col.append(jnp.transpose(jnp.broadcast_to(key, (LANES, LANES))))
        list_col.append(jnp.transpose(jnp.broadcast_to(safe, (LANES, LANES))))
        id_col.append(jnp.transpose(jnp.broadcast_to(got[1:2], (LANES, LANES))))

    slot_at = lax.broadcasted_iota(jnp.int32, (cap, LANES), 0)
    slot_list = jnp.zeros((cap, LANES), jnp.int32)
    pos_col = []
    for g in range(groups):
        rank = jnp.zeros((1, LANES), jnp.int32)
        for h in range(groups):
            less = (key_col[h] < key_row[g]).astype(jnp.int32)
            rank = rank + jnp.sum(less, axis=0, keepdims=True)
        rank = jnp.where(list_row[g] < owned, rank, cap + entries)
        hit = slot_at == rank
        place[:, pl.ds(g * LANES, LANES)] = hit.astype(F32).astype(BF16)
        slot_list = slot_list + jnp.where(hit, list_row[g] + 1, 0)
        pos_col.append(jnp.transpose(jnp.broadcast_to(rank, (LANES, LANES))))
    at_list = jnp.sum(slot_list, axis=1, keepdims=True) - 1

    for q in range(cap // LANES):
        total = jnp.zeros((1, LANES), jnp.int32)
        for g in range(groups):
            hit = pos_col[g] == lane + q * LANES
            total = total + jnp.sum(jnp.where(hit, id_col[g] + 1, 0), axis=0, keepdims=True)
        ids_out[pl.ds(q, 1), :] = total - 1
    for q in range(owned // LANES):
        total = jnp.zeros((1, LANES), jnp.int32)
        for g in range(groups):
            less = (list_col[g] < lane + q * LANES).astype(jnp.int32)
            total = total + jnp.sum(less, axis=0, keepdims=True)
        off_out[pl.ds(q, 1), :] = total

    res[...] = jnp.zeros_like(res)
    load_cent.wait()
    step = 256

    def centre(t, carry):
        base = pl.multiple_of(t * step, step)
        table = lax.broadcasted_iota(jnp.int32, (cap, step), 1) + base
        pick = (table == at_list).astype(F32).astype(BF16)
        for c in range(chunks):
            cols = pl.ds(c * wide, wide)
            hi, lo = split(cent_buf[pl.ds(base, step), cols])
            res[:, cols] -= dot(pick, hi) + dot(pick, lo)
        return carry

    lax.fori_loop(0, owned // step, centre, 0)

    load_rot.wait()

    def halve(t, carry):
        rows = pl.ds(pl.multiple_of(t * LANES, LANES), LANES)
        hi, lo = split(rot_buf[rows, :])
        rot_hi[rows, :] = hi
        rot_lo[rows, :] = lo
        return carry

    lax.fori_loop(0, width // LANES, halve, 0)
    out[...] = jnp.zeros_like(out)

    def turn(c, carry):
        pltpu.make_async_copy(recv.at[c, most], recv.at[c, most], recv_sem.at[c]).wait()
        own_rows(c).wait()
        cols = pl.ds(pl.multiple_of(c * wide, wide), wide)
        hi, lo = split(recv[c].reshape(entries, wide))
        spots = place[...]
        left = res[:, cols] + (dot(spots, hi) + dot(spots, lo))
        left_hi, left_lo = split(left)

        def tile(t, inner):
            at = pl.ds(pl.multiple_of(t * 256, 256), 256)
            r_hi = rot_hi[cols, at]
            r_lo = rot_lo[cols, at]
            out[:, at] += dot(left_hi, r_hi) + dot(left_lo, r_hi) + dot(left_hi, r_lo)
            return inner

        lax.fori_loop(0, width // 256, tile, 0)
        return carry

    lax.fori_loop(0, chunks, turn, 0)

    pltpu.make_async_copy(meta_in.at[most], meta_in.at[most], meta_send_sem).wait()
    for c in range(chunks):
        pltpu.make_async_copy(recv.at[c, most], recv.at[c, most], send_sem.at[c]).wait()


def full(embeddings, lists, row_ids, centroids, rotation):
    rows, width = embeddings.shape
    owned = centroids.shape[0]
    n = lax.axis_size("dev")
    cap = 2 * rows
    slots = max(8, cap // n)
    chunks = 4
    entries = n * slots
    me = lax.axis_index("dev")
    owner = lists // owned
    index = jnp.arange(rows, dtype=jnp.int32)
    earlier = index[None, :] < index[:, None]
    slot = jnp.sum((owner[None, :] == owner[:, None]) & earlier, axis=1).astype(jnp.int32)
    target = owner * slots + slot
    table = jnp.arange(entries, dtype=jnp.int32)
    match = target[None, :] == table[:, None]
    send = jnp.dot(match.astype(F32), embeddings, precision=lax.Precision.HIGH, preferred_element_type=F32)
    send = send.reshape(n, slots, width)
    per = LANES // slots
    own_lanes = (jnp.arange(LANES, dtype=jnp.int32) // slots) == lax.rem(me, per)

    def spread(values):
        picked = jnp.sum(jnp.where(match, values[None, :], 0), axis=1).astype(jnp.int32)
        return jnp.where(own_lanes[None, :], jnp.tile(picked.reshape(n, slots), (1, per)), 0)

    meta = jnp.zeros((n, 8, LANES), jnp.int32)
    meta = jnp.stack([spread(lists - owner * owned + 1), spread(row_ids)] + [jnp.zeros((n, LANES), jnp.int32)] * 6, axis=1)
    wide = width // chunks
    vmem = pl.BlockSpec(memory_space=pltpu.VMEM)
    hbm = pl.BlockSpec(memory_space=pltpu.HBM)
    packed, ids, offsets = pl.pallas_call(
        functools.partial(kernel, n, slots, chunks),
        out_shape=(
            jax.ShapeDtypeStruct((cap, width), F32),
            jax.ShapeDtypeStruct((cap // LANES, LANES), jnp.int32),
            jax.ShapeDtypeStruct((owned // LANES, LANES), jnp.int32),
        ),
        in_specs=[hbm, hbm, hbm, hbm],
        out_specs=(vmem, vmem, vmem),
        scratch_shapes=[
            pltpu.VMEM((chunks, n, slots, wide), F32),
            pltpu.VMEM((n, 8, LANES), jnp.int32),
            pltpu.VMEM((owned, width), F32),
            pltpu.VMEM((width, width), F32),
            pltpu.VMEM((width, width), BF16),
            pltpu.VMEM((width, width), BF16),
            pltpu.VMEM((cap, width), F32),
            pltpu.VMEM((cap, entries), BF16),
            pltpu.SemaphoreType.DMA((chunks,)),
            pltpu.SemaphoreType.DMA((chunks,)),
            pltpu.SemaphoreType.DMA,
            pltpu.SemaphoreType.DMA,
            pltpu.SemaphoreType.DMA((chunks + 1,)),
            pltpu.SemaphoreType.DMA((2,)),
        ],
        compiler_params=pltpu.CompilerParams(
            collective_id=1, has_side_effects=True, vmem_limit_bytes=48 * 1024 * 1024
        ),
    )(send, meta, centroids, rotation)
    return packed


def dot_t(a, b):
    return lax.dot_general(a, b, (((1,), (1,)), ((), ())), preferred_element_type=F32)


def hot(mask):
    return mask.astype(F32).astype(BF16)


def column_of(row):
    return jnp.transpose(jnp.broadcast_to(row, (LANES, LANES)))


def relayed_kernel(
    n, real, near, direct, pool,
    emb, lists, ids, cent, rot,
    out, ids_out, off_out, most_out,
    send_a, send_b, send_x, far_out, near_out, next_out, meta, recv, far_in, near_in, next_in, meta_in,
    part_1, part_2, part_3, cent_buf, rot_buf, rot_hi, rot_lo, res, left_hi, left_lo, place,
    send_sem, recv_sem, load_sem,
):
    me = lax.axis_index("dev")
    count, width = emb.shape
    cap = out.shape[0]
    owned = cent.shape[0]
    tall = width // LANES
    parts = count // LANES
    entries = n * real
    groups = entries // LANES
    members = n // LEVELS
    late = direct - near
    extra = real - direct
    block = far_in.shape[0]
    level = lax.div(me, members)
    inside = lax.rem(me, members)
    beside = level + 1 - 2 * lax.rem(level, 2)
    across = lax.rem(level + 2, LEVELS)
    corner = lax.rem(beside + 2, LEVELS)
    META, A, B, X, FAR, NEAR, NEXT = range(7)

    def flat(ref):
        return ref.reshape(ref.shape[0] * ref.shape[1] * tall, LANES) if len(ref.shape) == 4 else ref.reshape(ref.shape[0] * tall, LANES)

    recv_f, send_a_f, send_b_f, send_x_f = flat(recv), flat(send_a), flat(send_b), flat(send_x)
    far_out_f, near_out_f, next_out_f = flat(far_out), flat(near_out), flat(next_out)
    far_in_f, near_in_f, next_in_f = flat(far_in), flat(near_in), flat(next_in)
    part_1_f, part_2_f, part_3_f = flat(part_1), flat(part_2), flat(part_3)

    def tile_of(index):
        return pl.ds(pl.multiple_of(index * tall, 8), tall)

    load_cent = pltpu.make_async_copy(cent, cent_buf, load_sem.at[0])
    load_rot = pltpu.make_async_copy(rot, rot_buf, load_sem.at[1])
    barrier = pltpu.get_barrier_semaphore()

    def greet(k, carry):
        peer = lax.rem(me + k, n)
        pl.semaphore_signal(barrier, inc=1, device_id=(peer,), device_id_type=MESH)
        return carry

    lax.fori_loop(1, n, greet, 0)
    load_rot.start()
    load_cent.start()

    lane = lax.broadcasted_iota(jnp.int32, (1, LANES), 1)
    lanes = lax.broadcasted_iota(jnp.int32, (LANES, LANES), 1)
    subs = lax.broadcasted_iota(jnp.int32, (LANES, LANES), 0)
    ahead = subs < lanes

    list_of = [lists[r:r + 1, :] for r in range(parts)]
    id_of = [ids[r:r + 1, :] for r in range(parts)]
    owner_of = [lax.div(x, owned) for x in list_of]
    owner_col = [column_of(x) for x in owner_of]
    slot_of = []
    for r in range(parts):
        slot = jnp.zeros((1, LANES), jnp.int32)
        for q in range(r + 1):
            same = owner_col[q] == owner_of[r]
            if q == r:
                same = same & ahead
            slot = slot + jnp.sum(same.astype(jnp.int32), axis=0, keepdims=True)
        slot_of.append(slot)
    level_of = [lax.div(x, members) for x in owner_of]
    late_of = [slot_of[r] >= direct for r in range(parts)]
    home = [late_of[r] & (level_of[r] == level) for r in range(parts)]
    side = [late_of[r] & (level_of[r] == beside) for r in range(parts)]
    turn = [late_of[r] & (level_of[r] == corner) for r in range(parts)]
    gone = [late_of[r] & ((level_of[r] == across) | (level_of[r] == corner)) for r in range(parts)]
    seat = lax.broadcasted_iota(jnp.int32, (8, LANES), 0)
    triangle = hot(ahead)
    done = jnp.zeros((8, 1), F32)
    side_at, gone_at, turn_at = [], [], []
    for r in range(parts):
        mask = ((seat == 0) & side[r]) | ((seat == 1) & gone[r]) | ((seat == 2) & turn[r])
        flags = mask.astype(F32)
        index = (dot(flags.astype(BF16), triangle) + done).astype(jnp.int32)
        done = done + jnp.sum(flags, axis=1, keepdims=True)
        side_at.append(jnp.where(side[r], index[0:1], -1))
        gone_at.append(jnp.where(gone[r], index[1:2], -1))
        turn_at.append(jnp.where(turn[r], index[2:3], -1))
    worst = jnp.max(done, axis=0, keepdims=True).astype(jnp.int32)

    base_x = late * n
    base_far = base_x + extra * members
    base_near = base_far + block
    wanted = base_near + block
    table = lax.broadcasted_iota(jnp.int32, (wanted, LANES), 0)
    picks = []
    for r in range(parts):
        owner, slot = owner_of[r], slot_of[r]
        spot = (slot - direct) * members + lax.rem(owner, members)
        target = jnp.where((slot >= near) & (slot < direct), (slot - near) * n + owner, -1)
        target = jnp.where(home[r], base_x + spot, target)
        target = jnp.where((gone_at[r] >= 0) & (gone_at[r] < pool), base_far + gone_at[r], target)
        target = jnp.where((side_at[r] >= 0) & (side_at[r] < pool), base_near + side_at[r], target)
        picks.append(hot(table == target))
    pick = jnp.concatenate(picks, axis=1)
    for b in range(0, tall, 2):
        hi, lo = split(emb[:, b * LANES:(b + 2) * LANES])
        value = dot(pick, hi) + dot(pick, lo)
        for h in range(2):
            got = value[:, h * LANES:(h + 1) * LANES]
            send_a_f[pl.ds(b + h, late * n, stride=tall), :] = got[:base_x]
            send_x_f[pl.ds(b + h, extra * members, stride=tall), :] = got[base_x:base_far]
            far_out_f[pl.ds(b + h, block, stride=tall), :] = got[base_far:base_near]
            near_out_f[pl.ds(b + h, block, stride=tall), :] = got[base_near:]

    far_codes = jnp.zeros((8, LANES), F32)
    near_codes = jnp.zeros((8, LANES), F32)
    for r in range(parts):
        spot = (slot_of[r] - direct) * members + lax.rem(owner_of[r], members) + 1
        stay = gone[r] & (level_of[r] == across)
        first = jnp.where((seat == 0) & stay, spot, 0) + jnp.where((seat == 1) & turn[r], turn_at[r] + 1, 0)
        last = jnp.where(seat == 2, spot, 0)
        far_codes = far_codes + dot_t(first.astype(F32).astype(BF16), hot(subs == gone_at[r]))
        far_codes = far_codes + dot_t(last.astype(F32).astype(BF16), hot(subs == turn_at[r]))
        near_codes = near_codes + dot_t(last.astype(F32).astype(BF16), hot(subs == side_at[r]))
    far_out[pool] = far_codes - 1.0
    near_out[pool] = near_codes - 1.0
    blank = jnp.zeros((8, LANES), F32)
    for ref in (far_in, near_in, next_in):
        for k in range(pool + 1, block):
            ref[k] = blank

    owners = lax.broadcasted_iota(jnp.int32, (n, LANES), 0)
    high = jnp.zeros((n, LANES), F32)
    low = jnp.zeros((n, LANES), F32)
    for r in range(parts):
        mine = owners == owner_of[r]
        local = list_of[r] - owner_of[r] * owned + 1
        for values, shift in ((local, 0), (id_of[r], real)):
            spots = hot(subs == slot_of[r] + shift)
            upper = lax.div(values, 256)
            lower = values - upper * 256
            high = high + dot_t(jnp.where(mine, upper, 0).astype(F32).astype(BF16), spots)
            low = low + dot_t(jnp.where(mine, lower, 0).astype(F32).astype(BF16), spots)
    note = high.astype(jnp.int32) * 256 + low.astype(jnp.int32)
    meta[:, 0, :] = jnp.where(lane == 2 * real, worst, note)

    meta_in[pl.ds(me, 1)] = meta[pl.ds(me, 1)]
    for s in range(late):
        recv_f[tile_of((near + s) * n + me), :] = send_a_f[tile_of(s * n + me), :]
    for s in range(extra):
        recv_f[tile_of((direct + s) * n + me), :] = send_x_f[tile_of(s * members + inside), :]
    pl.semaphore_wait(barrier, n - 1)

    def post(src, dst, peer, at):
        pltpu.make_async_remote_copy(
            src_ref=src, dst_ref=dst, send_sem=send_sem.at[at], recv_sem=recv_sem.at[at],
            device_id=(peer,), device_id_type=MESH,
        ).start()

    def settle(ref, sem):
        pltpu.make_async_copy(ref, ref, sem).wait()

    def peer_of(k):
        peer, bit = 0, 1
        while bit < n:
            ours = lax.rem(lax.div(me, bit), 2)
            step = lax.rem(lax.div(k, bit), 2)
            peer = peer + bit * lax.rem(ours + step, 2)
            bit *= 2
        return peer

    def send_meta(k, carry):
        peer = peer_of(k)
        post(meta.at[peer], meta_in.at[me], peer, META)
        return carry

    def send_first(k, carry):
        peer = peer_of(k)
        post(send_a.at[:, peer], recv.at[pl.ds(near, late), me], peer, A)
        return carry

    def send_second(k, carry):
        peer = peer_of(k)
        post(send_b.at[:, peer], recv.at[pl.ds(0, near), me], peer, B)
        return carry

    def spread(ref, source):
        def one(k, carry):
            other = lax.rem(inside + k, members)
            post(ref.at[:, other], recv.at[pl.ds(direct, extra), source], level * members + other, X)
            return carry
        lax.fori_loop(1, members, one, 0)

    message = pl.ds(0, pool + 1)
    beside_dev = beside * members + inside
    across_dev = across * members + inside
    corner_dev = corner * members + inside

    lax.fori_loop(1, n, send_meta, 0)
    post(far_out.at[message], far_in.at[message], across_dev, FAR)
    post(near_out.at[message], near_in.at[message], beside_dev, NEAR)
    lax.fori_loop(1, n, send_first, 0)
    spread(send_x, me)

    span_meta = meta_in.at[pl.ds(0, n - 1)]
    settle(span_meta, recv_sem.at[META])

    got = meta_in[:, 0, :]
    if n < LANES:
        got = jnp.concatenate([got, jnp.zeros((LANES - n, LANES), jnp.int32)], axis=0)
    fields = jnp.transpose(got)
    most_out[...] = jnp.broadcast_to(jnp.max(fields[2 * real:2 * real + 1, :], axis=1, keepdims=True), (1, LANES))
    per = LANES // n
    rolled = [fields if k == 0 else pltpu.roll(fields, n * k, 1) for k in range(per)]

    def row_of(g, first):
        total = jnp.zeros((1, LANES), jnp.int32)
        for k in range(per):
            at = first + g * per + k
            total = total + rolled[k][at:at + 1, :]
        return total

    list_row, key_row, key_col, list_col, id_col = [], [], [], [], []
    for g in range(groups):
        found = row_of(g, 0) - 1
        safe = jnp.where(found >= 0, found, owned)
        entry = g * LANES + lane
        key = safe * entries + lax.rem(entry, n) * real + lax.div(entry, n)
        list_row.append(safe)
        key_row.append(key)
        key_col.append(column_of(key))
        list_col.append(column_of(safe))
        id_col.append(column_of(row_of(g, real)))

    slot_at = lax.broadcasted_iota(jnp.int32, (cap, LANES), 0)
    slot_list = jnp.zeros((cap, LANES), jnp.int32)
    pos_col = []
    for g in range(groups):
        rank = jnp.zeros((1, LANES), jnp.int32)
        for h in range(groups):
            less = (key_col[h] < key_row[g]).astype(jnp.int32)
            rank = rank + jnp.sum(less, axis=0, keepdims=True)
        rank = jnp.where(list_row[g] < owned, rank, cap + entries)
        hit = slot_at == rank
        place[:, pl.ds(g * LANES, LANES)] = hot(hit)
        slot_list = slot_list + jnp.where(hit, list_row[g] + 1, 0)
        pos_col.append(column_of(rank))
    at_list = jnp.sum(slot_list, axis=1, keepdims=True) - 1

    def piece(ref, first, rows, b):
        return ref[pl.ds(first * tall + b, rows, stride=tall), :]

    def pair(ref, first, rows, b):
        return split(jnp.concatenate([piece(ref, first, rows, b), piece(ref, first, rows, b + 1)], axis=1))

    seats = lax.broadcasted_iota(jnp.int32, (extra * members, block), 0)

    def expand(codes, source, target, forward):
        choose = hot(seats == codes[0][:, :block].astype(jnp.int32))
        if forward is not None:
            onward = lax.broadcasted_iota(jnp.int32, (block, block), 0) == codes[1][:, :block].astype(jnp.int32)
            choose = jnp.concatenate([choose, hot(onward)], axis=0)
        for b in range(0, tall, 2):
            hi, lo = pair(source, 0, block, b)
            value = dot(choose, hi) + dot(choose, lo)
            for h in range(2):
                part = value[:, h * LANES:(h + 1) * LANES]
                target[pl.ds(b + h, extra * members, stride=tall), :] = part[:extra * members]
                if forward is not None:
                    forward[pl.ds(b + h, block, stride=tall), :] = part[extra * members:]

    def keep(ref, source):
        for s in range(extra):
            recv_f[tile_of((direct + s) * n + source), :] = ref[tile_of(s * members + inside), :]

    settle(near_in.at[message], recv_sem.at[NEAR])
    expand([near_in[pool][2:3]], near_in_f, part_1_f, None)
    spread(part_1, beside_dev)
    keep(part_1_f, beside_dev)

    settle(far_in.at[message], recv_sem.at[FAR])
    codes = far_in[pool]
    expand([codes[0:1], codes[1:2]], far_in_f, part_2_f, next_out_f)
    next_out[pool] = codes
    post(next_out.at[message], next_in.at[message], beside_dev, NEXT)
    spread(part_2, across_dev)
    keep(part_2_f, across_dev)

    load_rot.wait()

    def halve(t, carry):
        at = pl.ds(pl.multiple_of(t * LANES, LANES), LANES)
        hi, lo = split(rot_buf[at, :])
        rot_hi[at, :] = hi
        rot_lo[at, :] = lo
        return carry

    lax.fori_loop(0, width // LANES, halve, 0)

    table = lax.broadcasted_iota(jnp.int32, (near * n, LANES), 0)
    pick = jnp.concatenate(
        [hot(table == jnp.where(slot_of[r] < near, slot_of[r] * n + owner_of[r], -1)) for r in range(parts)], axis=1
    )
    lines = pl.ds(0, near * n)
    for b in range(0, tall, 2):
        cols = pl.ds(b * LANES, 2 * LANES)
        hi, lo = split(emb[:, b * LANES:(b + 2) * LANES])
        hi, lo = split(dot(pick, hi) + dot(pick, lo))
        left_hi[lines, cols] = hi
        left_lo[lines, cols] = lo
    for b in range(0, tall, 2):
        at = pl.ds(b * LANES, 2 * LANES)
        r_hi = rot_hi[:, at]
        value = dot(left_hi[lines, :], r_hi) + dot(left_lo[lines, :], r_hi) + dot(left_hi[lines, :], rot_lo[:, at])
        for h in range(2):
            send_b_f[pl.ds(b + h, near * n, stride=tall), :] = value[:, h * LANES:(h + 1) * LANES]
    for s in range(near):
        recv_f[tile_of(s * n + me), :] = send_b_f[tile_of(s * n + me), :]
    lax.fori_loop(1, n, send_second, 0)

    for q in range(cap // LANES):
        total = jnp.zeros((1, LANES), jnp.int32)
        for g in range(groups):
            hit = pos_col[g] == lane + q * LANES
            total = total + jnp.sum(jnp.where(hit, id_col[g] + 1, 0), axis=0, keepdims=True)
        ids_out[pl.ds(q, 1), :] = total - 1
    for q in range(owned // LANES):
        total = jnp.zeros((1, LANES), jnp.int32)
        for g in range(groups):
            less = (list_col[g] < lane + q * LANES).astype(jnp.int32)
            total = total + jnp.sum(less, axis=0, keepdims=True)
        off_out[pl.ds(q, 1), :] = total

    settle(next_in.at[message], recv_sem.at[NEXT])
    expand([next_in[pool][2:3]], next_in_f, part_3_f, None)
    spread(part_3, corner_dev)
    keep(part_3_f, corner_dev)

    res[...] = jnp.zeros_like(res)
    load_cent.wait()
    step = 256

    def centre(t, carry):
        base = pl.multiple_of(t * step, step)
        table = lax.broadcasted_iota(jnp.int32, (cap, step), 1) + base
        pick = hot(table == at_list)
        for c in range(width // step):
            cols = pl.ds(c * step, step)
            hi, lo = split(cent_buf[pl.ds(base, step), cols])
            res[:, cols] -= dot(pick, hi) + dot(pick, lo)
        return carry

    lax.fori_loop(0, owned // step, centre, 0)

    span_a = recv.at[pl.ds(near, late), pl.ds(0, n - 1)]
    settle(span_a, recv_sem.at[A])
    span_x = recv_f.at[pl.ds(0, LEVELS * extra * (members - 1) * tall)]
    settle(span_x, recv_sem.at[X])
    rest = entries - near * n
    for b in range(0, tall, 2):
        cols = pl.ds(b * LANES, 2 * LANES)
        hi, lo = pair(recv_f, near * n, rest, b)
        spots = place[:, near * n:]
        hi, lo = split(res[:, cols] + dot(spots, hi) + dot(spots, lo))
        left_hi[:, cols] = hi
        left_lo[:, cols] = lo

    def tile(t, carry):
        at = pl.ds(pl.multiple_of(t * 256, 256), 256)
        r_hi = rot_hi[:, at]
        out[:, at] = dot(left_hi[...], r_hi) + dot(left_lo[...], r_hi) + dot(left_hi[...], rot_lo[:, at])
        return carry

    lax.fori_loop(0, width // 256, tile, 0)

    span_b = recv.at[pl.ds(0, near), pl.ds(0, n - 1)]
    settle(span_b, recv_sem.at[B])
    for b in range(0, tall, 2):
        cols = pl.ds(b * LANES, 2 * LANES)
        hi, lo = pair(recv_f, 0, near * n, b)
        spots = place[:, :near * n]
        out[:, cols] += dot(spots, hi) + dot(spots, lo)

    settle(span_meta, send_sem.at[META])
    settle(span_a, send_sem.at[A])
    settle(span_b, send_sem.at[B])
    settle(span_x, send_sem.at[X])
    settle(far_in.at[message], send_sem.at[FAR])
    settle(near_in.at[message], send_sem.at[NEAR])
    settle(next_in.at[message], send_sem.at[NEXT])


def emit_kernel(rows, ids, offsets, rows_out, ids_out, off_out, sem):
    moves = [
        pltpu.make_async_copy(src, dst, sem.at[k])
        for k, (src, dst) in enumerate(((rows, rows_out), (ids, ids_out), (offsets, off_out)))
    ]
    for move in moves:
        move.start()
    for move in moves:
        move.wait()


def emit(rows, ids, offsets):
    vmem = pl.BlockSpec(memory_space=pltpu.VMEM)
    hbm = pl.BlockSpec(memory_space=pltpu.HBM)
    return pl.pallas_call(
        emit_kernel,
        out_shape=tuple(jax.ShapeDtypeStruct(x.shape, x.dtype) for x in (rows, ids, offsets)),
        in_specs=[vmem] * 3,
        out_specs=(hbm,) * 3,
        scratch_shapes=[pltpu.SemaphoreType.DMA((3,))],
    )(rows, ids, offsets)


LEVELS = 4
POOL = 46


def local(embeddings, lists, row_ids, centroids, rotation):
    row_count, width = embeddings.shape
    owned = centroids.shape[0]
    n = lax.axis_size("dev")
    cap = 2 * row_count
    real = cap // n
    near = LANES // n
    direct = (7 * real + 8) // 16
    late, extra = direct - near, real - direct
    members = n // LEVELS
    pool = POOL
    block = -(-(pool + 1) // 16) * 16
    tall = width // LANES
    by_lane = (row_count // LANES, LANES)
    vmem = pl.BlockSpec(memory_space=pltpu.VMEM)
    hbm = pl.BlockSpec(memory_space=pltpu.HBM)

    def rows_of(*lead):
        return pltpu.VMEM((*lead, tall, LANES), F32)

    packed, ids, offsets, most = pl.pallas_call(
        functools.partial(relayed_kernel, n, real, near, direct, pool),
        out_shape=(
            jax.ShapeDtypeStruct((cap, width), F32),
            jax.ShapeDtypeStruct((cap // LANES, LANES), jnp.int32),
            jax.ShapeDtypeStruct((owned // LANES, LANES), jnp.int32),
            jax.ShapeDtypeStruct((1, LANES), jnp.int32),
        ),
        in_specs=[vmem] * 3 + [hbm] * 2,
        out_specs=(vmem,) * 4,
        scratch_shapes=[
            rows_of(late, n), rows_of(near, n), rows_of(extra, members), rows_of(block), rows_of(block), rows_of(block),
            pltpu.VMEM((n, 1, LANES), jnp.int32),
            rows_of(real, n), rows_of(block), rows_of(block), rows_of(block),
            pltpu.VMEM((n, 1, LANES), jnp.int32),
            rows_of(extra, members), rows_of(extra, members), rows_of(extra, members),
            pltpu.VMEM((owned, width), F32),
            pltpu.VMEM((width, width), F32),
            pltpu.VMEM((width, width), BF16),
            pltpu.VMEM((width, width), BF16),
            pltpu.VMEM((cap, width), F32),
            pltpu.VMEM((cap, width), BF16),
            pltpu.VMEM((cap, width), BF16),
            pltpu.VMEM((cap, n * real), BF16),
            pltpu.SemaphoreType.DMA((7,)),
            pltpu.SemaphoreType.DMA((7,)),
            pltpu.SemaphoreType.DMA((2,)),
        ],
        compiler_params=pltpu.CompilerParams(
            collective_id=0, has_side_effects=True, vmem_limit_bytes=48 * 1024 * 1024
        ),
    )(embeddings, lists.reshape(by_lane), row_ids.reshape(by_lane), centroids, rotation)
    packed, ids, offsets = lax.cond(
        most[0, 0] > pool,
        lambda: (full(embeddings, lists, row_ids, centroids, rotation), ids, offsets),
        lambda: emit(packed, ids, offsets),
    )
    return packed, ids.reshape(-1), offsets.reshape(-1)


def solution(mesh):
    in_specs = (P("dev", None), P("dev"), P("dev"), P("dev", None), P())
    out_specs = (P("dev", None), P("dev"), P("dev"))
    return jax.shard_map(local, mesh=mesh, in_specs=in_specs, out_specs=out_specs, check_vma=False)
```

time: 56 us -> 51.6 us (0.921); the launches traced: 55 us -> 51.5 us
  Pallas kernels: 51.3 us -> 46.3 us
  local copies, waits for them, and re-layouts: 1.19 us -> 4.35 us
  other arithmetic: 1.53 us -> 0 us
    pallas_call x1 -> x2, Pallas kernels: 51.3 us -> 46.3 us  [the longest x1 45 us: local(): pl.pallas_call(functools.partial(relayed_kernel, n, real, near, direct, p...]
    unnamed x8 -> x9, local copies, waits for them, and re-layouts: 1.19 us -> 4.35 us
    select_n x1 -> x0, other arithmetic: 1.53 us -> none  [local(): packed = jnp.where(ids.reshape(-1)[:, None] >= 0, packed, 0.0)]
where the time goes in v1:
time: 51.6 us; the launch traced here: 51.5 us
  Pallas kernels  46.3 us (90%)
  local copies, waits for them, and re-layouts  4.35 us (8%)
  between operations  0.73 us (1%)
    pallas_call x1, Pallas kernels, local(): pl.pallas_call(functools.partial(relayed_kernel, n, real, near, direct, p...  45 us
    unnamed x9, local copies, waits for them, and re-layouts  4.35 us
    pallas_call x1, Pallas kernels, emit(): pl.pallas_call(emit_kernel, out_shape=tuple((jax.ShapeDtypeStruct(x.shape...  1.37 us

profile of v1, /device:TPU:0, one launch (start us, length us, event | category | flops | bytes accessed | tf_op | source)
XLA Modules:
  0.0 51.5 jit_solution(1723950000282104919)
XLA Ops:
  0.6 0.0 copy-start
  0.6 0.0 copy-start.1
  0.7 0.0 copy-start.2
  0.7 45.0 %shard_map.76 = (f32[512,1024]{1,0:T(8,128)S(1)}, s32[4,128]{1,0:T(4,128)S(1)}, s32[16,128]{1,0:T(8,128)S(1)}, s32[1,128]{1,0:T(1,128)S(1)}) custom-call(f32[256,1024]{1,0:T(8,128)} %emb.1, s32[2,128]{1,0:T(2,128)} %bitcast.16, s32[2,128]{1,0:T(2,128)} %bitcast.17, f32[2048,1024]{1,0:T(8,128)} %cent.1, f32[1024,1024]{1,0:T(8,128)} %rot.1), custom_call_target="tpu_custom_call" | custom-call | tf_op jit(solution)/shard_map/pallas_call | solution.py:705
  45.7 0.0 copy-done
  45.7 0.0 copy-done.1
  45.7 0.0 copy-done.2
  45.7 1.4 %conditional.1 = ((f32[512,1024]{1,0:T(8,128)}, s32[4,128]{1,0:T(4,128)S(1)}, s32[16,128]{1,0:T(8,128)S(1)}), s32[4,128]{1,0:T(4,128)S(1)}, s32[16,128]{1,0:T(8,128)S(1)}) conditional(s32[]{:T(128)} %bitcast.5, (f32[512,1024]{1,0:T(8,128)S(1)}, s32[4,128]{1,0:T(4,128)S(1)}, s32[16,128]{1,0:T(8,128)S(1)}) %tuple.19, (s32[256]{0:T(256)S(1)}, ...), branch_computations={%region_0.0_spmd, %region_1.5_spmd} | conditional | flops 806531968 | bytes 3510831 | solution.py:737
  45.7 1.4 %branch_0_fun.1 = (f32[512,1024]{1,0:T(8,128)}, s32[4,128]{1,0:T(4,128)S(1)}, s32[16,128]{1,0:T(8,128)S(1)}) custom-call(f32[512,1024]{1,0:T(8,128)S(1)} %get-tuple-element.25.rows, s32[4,128]{1,0:T(4,128)S(1)} %get-tuple-element.26.ids, s32[16,128]{1,0:T(8,128)S(1)} %get-tuple-element.27.offsets), custom_call_target="tpu_custom_call" | custom-call | tf_op jit(solution)/shard_map/cond/branch_0_fun/pallas_call | solution.py:672
  47.1 3.2 %copy.29 = f32[512,1024]{1,0:T(8,128)} copy(f32[512,1024]{1,0:T(8,128)} %get-tuple-element.75) | data formatting | bytes 4194304
  50.3 0.6 %copy.30 = s32[512]{0:T(512)} copy(s32[512]{0:T(512)S(1)} %bitcast.15) | data formatting | bytes 4096
  50.9 0.6 %copy.31 = s32[2048]{0:T(1024)} copy(s32[2048]{0:T(1024)S(1)} %bitcast.14) | data formatting | bytes 16384
  (2 shorter events, 0.0 us)
Async XLA Ops:
  0.6 45.1 %copy-start = (f32[256,1024]{1,0:T(8,128)S(1)}, f32[256,1024]{1,0:T(8,128)}, u32[]{:S(2)}) copy-start(f32[256,1024]{1,0:T(8,128)} %emb.1) | copy-start | bytes 3145732
  0.6 45.1 %copy-start.1 = (s32[256]{0:T(256)S(1)}, s32[256]{0:T(256)}, u32[]{:S(2)}) copy-start(s32[256]{0:T(256)} %param.8) | copy-start | bytes 3076
  0.7 45.1 %copy-start.2 = (s32[256]{0:T(256)S(1)}, s32[256]{0:T(256)}, u32[]{:S(2)}) copy-start(s32[256]{0:T(256)} %param.9) | copy-start | bytes 3076

commit v2 on v1

--- a/solution.py
+++ b/solution.py
@@ -265,9 +265,9 @@
 
 def relayed_kernel(
     n, real, near, direct, pool,
-    emb, lists, ids, cent, rot,
-    out, ids_out, off_out, most_out,
-    send_a, send_b, send_x, far_out, near_out, next_out, meta, recv, far_in, near_in, next_in, meta_in,
+    emb_hbm, lists_hbm, ids_hbm, cent, rot,
+    out, last_hi, last_lo, last_place, ids_out, off_out, most_out,
+    emb, lists, ids, turned_hi, turned_lo, send_a, send_b, send_x, far_out, near_out, next_out, meta, recv, far_in, near_in, next_in, meta_in,
     part_1, part_2, part_3, cent_buf, rot_buf, rot_hi, rot_lo, res, left_hi, left_lo, place,
     send_sem, recv_sem, load_sem,
 ):
@@ -311,8 +311,15 @@
         return carry
 
     lax.fori_loop(1, n, greet, 0)
+    loads = [
+        pltpu.make_async_copy(src, dst, load_sem.at[2 + k])
+        for k, (src, dst) in enumerate(((lists_hbm, lists), (ids_hbm, ids), (emb_hbm, emb)))
+    ]
+    for load in loads:
+        load.start()
     load_rot.start()
-    load_cent.start()
+    for load in loads:
+        load.wait()
 
     lane = lax.broadcasted_iota(jnp.int32, (1, LANES), 1)
     lanes = lax.broadcasted_iota(jnp.int32, (LANES, LANES), 1)
@@ -352,30 +359,22 @@
         turn_at.append(jnp.where(turn[r], index[2:3], -1))
     worst = jnp.max(done, axis=0, keepdims=True).astype(jnp.int32)
 
-    base_x = late * n
-    base_far = base_x + extra * members
-    base_near = base_far + block
-    wanted = base_near + block
-    table = lax.broadcasted_iota(jnp.int32, (wanted, LANES), 0)
+    table = lax.broadcasted_iota(jnp.int32, (2 * block, LANES), 0)
     picks = []
     for r in range(parts):
-        owner, slot = owner_of[r], slot_of[r]
-        spot = (slot - direct) * members + lax.rem(owner, members)
-        target = jnp.where((slot >= near) & (slot < direct), (slot - near) * n + owner, -1)
-        target = jnp.where(home[r], base_x + spot, target)
-        target = jnp.where((gone_at[r] >= 0) & (gone_at[r] < pool), base_far + gone_at[r], target)
-        target = jnp.where((side_at[r] >= 0) & (side_at[r] < pool), base_near + side_at[r], target)
+        target = jnp.where((gone_at[r] >= 0) & (gone_at[r] < pool), gone_at[r], -1)
+        target = jnp.where((side_at[r] >= 0) & (side_at[r] < pool), block + side_at[r], target)
         picks.append(hot(table == target))
     pick = jnp.concatenate(picks, axis=1)
     for b in range(0, tall, 2):
         hi, lo = split(emb[:, b * LANES:(b + 2) * LANES])
+        left_hi[pl.ds(0, count), pl.ds(b * LANES, 2 * LANES)] = hi
+        left_lo[pl.ds(0, count), pl.ds(b * LANES, 2 * LANES)] = lo
         value = dot(pick, hi) + dot(pick, lo)
         for h in range(2):
             got = value[:, h * LANES:(h + 1) * LANES]
-            send_a_f[pl.ds(b + h, late * n, stride=tall), :] = got[:base_x]
-            send_x_f[pl.ds(b + h, extra * members, stride=tall), :] = got[base_x:base_far]
-            far_out_f[pl.ds(b + h, block, stride=tall), :] = got[base_far:base_near]
-            near_out_f[pl.ds(b + h, block, stride=tall), :] = got[base_near:]
+            far_out_f[pl.ds(b + h, block, stride=tall), :] = got[:block]
+            near_out_f[pl.ds(b + h, block, stride=tall), :] = got[block:]
 
     far_codes = jnp.zeros((8, LANES), F32)
     near_codes = jnp.zeros((8, LANES), F32)
@@ -410,10 +409,6 @@
     meta[:, 0, :] = jnp.where(lane == 2 * real, worst, note)
 
     meta_in[pl.ds(me, 1)] = meta[pl.ds(me, 1)]
-    for s in range(late):
-        recv_f[tile_of((near + s) * n + me), :] = send_a_f[tile_of(s * n + me), :]
-    for s in range(extra):
-        recv_f[tile_of((direct + s) * n + me), :] = send_x_f[tile_of(s * members + inside), :]
     pl.semaphore_wait(barrier, n - 1)
 
     def post(src, dst, peer, at):
@@ -464,8 +459,60 @@
     lax.fori_loop(1, n, send_meta, 0)
     post(far_out.at[message], far_in.at[message], across_dev, FAR)
     post(near_out.at[message], near_in.at[message], beside_dev, NEAR)
+    load_rot.wait()
+    load_cent.start()
+
+    def halve(t, carry):
+        at = pl.ds(pl.multiple_of(t * LANES, LANES), LANES)
+        hi, lo = split(rot_buf[at, :])
+        rot_hi[at, :] = hi
+        rot_lo[at, :] = lo
+        return carry
+
+    lax.fori_loop(0, width // LANES, halve, 0)
+
+    def turn_rows(lines):
+        def turned(t, carry):
+            at = pl.ds(pl.multiple_of(t * 256, 256), 256)
+            r_hi = rot_hi[:, at]
+            value = dot(left_hi[lines, :], r_hi) + dot(left_lo[lines, :], r_hi) + dot(left_hi[lines, :], rot_lo[:, at])
+            hi, lo = split(value)
+            turned_hi[lines, at] = hi
+            turned_lo[lines, at] = lo
+            return carry
+
+        lax.fori_loop(0, width // 256, turned, 0)
+
+    turn_rows(pl.ds(0, count))
+    base_x = late * n
+    base_b = base_x + extra * members
+    wanted = base_b + near * n
+    table = lax.broadcasted_iota(jnp.int32, (wanted, LANES), 0)
+    picks = []
+    for r in range(parts):
+        owner, slot = owner_of[r], slot_of[r]
+        spot = (slot - direct) * members + lax.rem(owner, members)
+        target = jnp.where(slot < direct, (slot - near) * n + owner, -1)
+        target = jnp.where(slot < near, base_b + slot * n + owner, target)
+        target = jnp.where(home[r], base_x + spot, target)
+        picks.append(hot(table == target))
+    pick = jnp.concatenate(picks, axis=1)
+    for b in range(0, tall, 2):
+        cols = pl.ds(b * LANES, 2 * LANES)
+        value = dot(pick, turned_hi[:, cols]) + dot(pick, turned_lo[:, cols])
+        for h in range(2):
+            got = value[:, h * LANES:(h + 1) * LANES]
+            send_a_f[pl.ds(b + h, late * n, stride=tall), :] = got[:base_x]
+            send_x_f[pl.ds(b + h, extra * members, stride=tall), :] = got[base_x:base_b]
+            send_b_f[pl.ds(b + h, near * n, stride=tall), :] = got[base_b:]
     lax.fori_loop(1, n, send_first, 0)
     spread(send_x, me)
+    for s in range(late):
+        recv_f[tile_of((near + s) * n + me), :] = send_a_f[tile_of(s * n + me), :]
+    for s in range(near):
+        recv_f[tile_of(s * n + me), :] = send_b_f[tile_of(s * n + me), :]
+    for s in range(extra):
+        recv_f[tile_of((direct + s) * n + me), :] = send_x_f[tile_of(s * members + inside), :]
 
     span_meta = meta_in.at[pl.ds(0, n - 1)]
     settle(span_meta, recv_sem.at[META])
@@ -520,13 +567,25 @@
 
     seats = lax.broadcasted_iota(jnp.int32, (extra * members, block), 0)
 
-    def expand(codes, source, target, forward):
+    def expand(codes, source, target, forward, raw):
         choose = hot(seats == codes[0][:, :block].astype(jnp.int32))
         if forward is not None:
             onward = lax.broadcasted_iota(jnp.int32, (block, block), 0) == codes[1][:, :block].astype(jnp.int32)
             choose = jnp.concatenate([choose, hot(onward)], axis=0)
+        lines = pl.ds(0, block)
+        if raw:
+            for b in range(0, tall, 2):
+                cols = pl.ds(b * LANES, 2 * LANES)
+                hi, lo = pair(source, 0, block, b)
+                left_hi[lines, cols] = hi
+                left_lo[lines, cols] = lo
+            turn_rows(lines)
         for b in range(0, tall, 2):
-            hi, lo = pair(source, 0, block, b)
+            if raw:
+                cols = pl.ds(b * LANES, 2 * LANES)
+                hi, lo = turned_hi[lines, cols], turned_lo[lines, cols]
+            else:
+                hi, lo = pair(source, 0, block, b)
             value = dot(choose, hi) + dot(choose, lo)
             for h in range(2):
                 part = value[:, h * LANES:(h + 1) * LANES]
@@ -539,48 +598,18 @@
             recv_f[tile_of((direct + s) * n + source), :] = ref[tile_of(s * members + inside), :]
 
     settle(near_in.at[message], recv_sem.at[NEAR])
-    expand([near_in[pool][2:3]], near_in_f, part_1_f, None)
+    expand([near_in[pool][2:3]], near_in_f, part_1_f, None, True)
     spread(part_1, beside_dev)
     keep(part_1_f, beside_dev)
 
     settle(far_in.at[message], recv_sem.at[FAR])
     codes = far_in[pool]
-    expand([codes[0:1], codes[1:2]], far_in_f, part_2_f, next_out_f)
+    expand([codes[0:1], codes[1:2]], far_in_f, part_2_f, next_out_f, True)
     next_out[pool] = codes
     post(next_out.at[message], next_in.at[message], beside_dev, NEXT)
     spread(part_2, across_dev)
     keep(part_2_f, across_dev)
 
-    load_rot.wait()
-
-    def halve(t, carry):
-        at = pl.ds(pl.multiple_of(t * LANES, LANES), LANES)
-        hi, lo = split(rot_buf[at, :])
-        rot_hi[at, :] = hi
-        rot_lo[at, :] = lo
-        return carry
-
-    lax.fori_loop(0, width // LANES, halve, 0)
-
-    table = lax.broadcasted_iota(jnp.int32, (near * n, LANES), 0)
-    pick = jnp.concatenate(
-        [hot(table == jnp.where(slot_of[r] < near, slot_of[r] * n + owner_of[r], -1)) for r in range(parts)], axis=1
-    )
-    lines = pl.ds(0, near * n)
-    for b in range(0, tall, 2):
-        cols = pl.ds(b * LANES, 2 * LANES)
-        hi, lo = split(emb[:, b * LANES:(b + 2) * LANES])
-        hi, lo = split(dot(pick, hi) + dot(pick, lo))
-        left_hi[lines, cols] = hi
-        left_lo[lines, cols] = lo
-    for b in range(0, tall, 2):
-        at = pl.ds(b * LANES, 2 * LANES)
-        r_hi = rot_hi[:, at]
-        value = dot(left_hi[lines, :], r_hi) + dot(left_lo[lines, :], r_hi) + dot(left_hi[lines, :], rot_lo[:, at])
-        for h in range(2):
-            send_b_f[pl.ds(b + h, near * n, stride=tall), :] = value[:, h * LANES:(h + 1) * LANES]
-    for s in range(near):
-        recv_f[tile_of(s * n + me), :] = send_b_f[tile_of(s * n + me), :]
     lax.fori_loop(1, n, send_second, 0)
 
     for q in range(cap // LANES):
@@ -596,11 +625,6 @@
             total = total + jnp.sum(less, axis=0, keepdims=True)
         off_out[pl.ds(q, 1), :] = total
 
-    settle(next_in.at[message], recv_sem.at[NEXT])
-    expand([next_in[pool][2:3]], next_in_f, part_3_f, None)
-    spread(part_3, corner_dev)
-    keep(part_3_f, corner_dev)
-
     res[...] = jnp.zeros_like(res)
     load_cent.wait()
     step = 256
@@ -616,6 +640,25 @@
         return carry
 
     lax.fori_loop(0, owned // step, centre, 0)
+
+    settle(next_in.at[message], recv_sem.at[NEXT])
+    expand([next_in[pool][2:3]], next_in_f, part_3_f, None, False)
+    spread(part_3, corner_dev)
+    keep(part_3_f, corner_dev)
+
+    for b in range(0, tall, 2):
+        cols = pl.ds(b * LANES, 2 * LANES)
+        hi, lo = split(res[:, cols])
+        left_hi[:, cols] = hi
+        left_lo[:, cols] = lo
+
+    def tile(t, carry):
+        at = pl.ds(pl.multiple_of(t * 256, 256), 256)
+        r_hi = rot_hi[:, at]
+        out[:, at] = dot(left_hi[...], r_hi) + dot(left_lo[...], r_hi) + dot(left_hi[...], rot_lo[:, at])
+        return carry
+
+    lax.fori_loop(0, width // 256, tile, 0)
 
     span_a = recv.at[pl.ds(near, late), pl.ds(0, n - 1)]
     settle(span_a, recv_sem.at[A])
@@ -626,25 +669,16 @@
         cols = pl.ds(b * LANES, 2 * LANES)
         hi, lo = pair(recv_f, near * n, rest, b)
         spots = place[:, near * n:]
-        hi, lo = split(res[:, cols] + dot(spots, hi) + dot(spots, lo))
-        left_hi[:, cols] = hi
-        left_lo[:, cols] = lo
-
-    def tile(t, carry):
-        at = pl.ds(pl.multiple_of(t * 256, 256), 256)
-        r_hi = rot_hi[:, at]
-        out[:, at] = dot(left_hi[...], r_hi) + dot(left_lo[...], r_hi) + dot(left_hi[...], rot_lo[:, at])
-        return carry
-
-    lax.fori_loop(0, width // 256, tile, 0)
+        out[:, cols] += dot(spots, hi) + dot(spots, lo)
 
     span_b = recv.at[pl.ds(0, near), pl.ds(0, n - 1)]
     settle(span_b, recv_sem.at[B])
     for b in range(0, tall, 2):
         cols = pl.ds(b * LANES, 2 * LANES)
         hi, lo = pair(recv_f, 0, near * n, b)
-        spots = place[:, :near * n]
-        out[:, cols] += dot(spots, hi) + dot(spots, lo)
+        last_hi[:, cols] = hi
+        last_lo[:, cols] = lo
+    last_place[...] = place[:, :near * n]
 
     settle(span_meta, send_sem.at[META])
     settle(span_a, send_sem.at[A])
@@ -655,27 +689,37 @@
     settle(next_in.at[message], send_sem.at[NEXT])
 
 
-def emit_kernel(rows, ids, offsets, rows_out, ids_out, off_out, sem):
+def finish_kernel(rows, hi, lo, place, ids, offsets, rows_out, ids_out, off_out, buf, sem):
+    wide = 256
+    tiles = rows.shape[1] // wide
     moves = [
-        pltpu.make_async_copy(src, dst, sem.at[k])
-        for k, (src, dst) in enumerate(((rows, rows_out), (ids, ids_out), (offsets, off_out)))
+        pltpu.make_async_copy(ids, ids_out, sem.at[tiles]),
+        pltpu.make_async_copy(offsets, off_out, sem.at[tiles + 1]),
     ]
     for move in moves:
         move.start()
+    for t in range(tiles):
+        cols = pl.ds(t * wide, wide)
+        buf[t] = rows[:, cols] + dot(place[...], hi[:, cols]) + dot(place[...], lo[:, cols])
+        move = pltpu.make_async_copy(buf.at[t], rows_out.at[:, cols], sem.at[t])
+        move.start()
+        moves.append(move)
     for move in moves:
         move.wait()
 
 
-def emit(rows, ids, offsets):
+def finish(rows, hi, lo, place, ids, offsets):
     vmem = pl.BlockSpec(memory_space=pltpu.VMEM)
     hbm = pl.BlockSpec(memory_space=pltpu.HBM)
+    cap, width = rows.shape
     return pl.pallas_call(
-        emit_kernel,
+        finish_kernel,
         out_shape=tuple(jax.ShapeDtypeStruct(x.shape, x.dtype) for x in (rows, ids, offsets)),
-        in_specs=[vmem] * 3,
+        in_specs=[vmem] * 6,
         out_specs=(hbm,) * 3,
-        scratch_shapes=[pltpu.SemaphoreType.DMA((3,))],
-    )(rows, ids, offsets)
+        scratch_shapes=[pltpu.VMEM((width // 256, cap, 256), F32), pltpu.SemaphoreType.DMA((width // 256 + 2,))],
+        compiler_params=pltpu.CompilerParams(vmem_limit_bytes=16 * 1024 * 1024),
+    )(rows, hi, lo, place, ids, offsets)
 
 
 LEVELS = 4
@@ -702,17 +746,25 @@
     def rows_of(*lead):
         return pltpu.VMEM((*lead, tall, LANES), F32)
 
-    packed, ids, offsets, most = pl.pallas_call(
+    packed, hi, lo, place, ids, offsets, most = pl.pallas_call(
         functools.partial(relayed_kernel, n, real, near, direct, pool),
         out_shape=(
             jax.ShapeDtypeStruct((cap, width), F32),
+            jax.ShapeDtypeStruct((near * n, width), BF16),
+            jax.ShapeDtypeStruct((near * n, width), BF16),
+            jax.ShapeDtypeStruct((cap, near * n), BF16),
             jax.ShapeDtypeStruct((cap // LANES, LANES), jnp.int32),
             jax.ShapeDtypeStruct((owned // LANES, LANES), jnp.int32),
             jax.ShapeDtypeStruct((1, LANES), jnp.int32),
         ),
-        in_specs=[vmem] * 3 + [hbm] * 2,
-        out_specs=(vmem,) * 4,
+        in_specs=[hbm] * 5,
+        out_specs=(vmem,) * 7,
         scratch_shapes=[
+            pltpu.VMEM((row_count, width), F32),
+            pltpu.VMEM(by_lane, jnp.int32),
+            pltpu.VMEM(by_lane, jnp.int32),
+            pltpu.VMEM((row_count, width), BF16),
+            pltpu.VMEM((row_count, width), BF16),
             rows_of(late, n), rows_of(near, n), rows_of(extra, members), rows_of(block), rows_of(block), rows_of(block),
             pltpu.VMEM((n, 1, LANES), jnp.int32),
             rows_of(real, n), rows_of(block), rows_of(block), rows_of(block),
@@ -728,17 +780,18 @@
             pltpu.VMEM((cap, n * real), BF16),
             pltpu.SemaphoreType.DMA((7,)),
             pltpu.SemaphoreType.DMA((7,)),
-            pltpu.SemaphoreType.DMA((2,)),
+            pltpu.SemaphoreType.DMA((5,)),
         ],
         compiler_params=pltpu.CompilerParams(
             collective_id=0, has_side_effects=True, vmem_limit_bytes=48 * 1024 * 1024
         ),
     )(embeddings, lists.reshape(by_lane), row_ids.reshape(by_lane), centroids, rotation)
-    packed, ids, offsets = lax.cond(
+    packed, hi, lo = lax.cond(
         most[0, 0] > pool,
-        lambda: (full(embeddings, lists, row_ids, centroids, rotation), ids, offsets),
-        lambda: emit(packed, ids, offsets),
+        lambda: (full(embeddings, lists, row_ids, centroids, rotation), jnp.zeros_like(hi), jnp.zeros_like(lo)),
+        lambda: (packed, hi, lo),
     )
+    packed, ids, offsets = finish(packed, hi, lo, place, ids, offsets)
     return packed, ids.reshape(-1), offsets.reshape(-1)
 
 

time: 51.6 us -> 44.3 us (0.86)
  local copies, waits for them, and re-layouts: 4.35 us -> 0.01 us
  Pallas kernels: 46.3 us -> 43.4 us
    unnamed x9 -> x4, local copies, waits for them, and re-layouts: 4.35 us -> 0.01 us
    pallas_call x1, Pallas kernels: 45 us -> 40.6 us  [local(): pl.pallas_call(functools.partial(relayed_kernel, n, real, near, direct, p...]
    pallas_call x1, Pallas kernels: 1.37 us -> 2.76 us  [finish(): pl.pallas_call(finish_kernel, out_shape=tuple((jax.ShapeDtypeStruct(x.sha...]
where the time goes in v2:
time: 44.3 us; the launch traced here: 44.1 us
  Pallas kernels  43.4 us (98%)
  between operations  0.71 us (2%)
    pallas_call x1, Pallas kernels, local(): pl.pallas_call(functools.partial(relayed_kernel, n, real, near, direct, p...  40.6 us
    pallas_call x1, Pallas kernels, finish(): pl.pallas_call(finish_kernel, out_shape=tuple((jax.ShapeDtypeStruct(x.sha...  2.76 us

profile of v2, /device:TPU:0, one launch (start us, length us, event | category | flops | bytes accessed | tf_op | source)
XLA Modules:
  0.0 44.1 jit_solution(10824533060912998599)
XLA Ops:
  0.6 0.0 copy-start
  0.6 0.0 copy-start.1
  0.6 40.6 %shard_map.76 = (f32[512,1024]{1,0:T(8,128)S(1)}, bf16[128,1024]{1,0:T(8,128)(2,1)S(1)}, bf16[128,1024]{1,0:T(8,128)(2,1)}, bf16[512,128]{1,0:T(8,128)(2,1)S(1)}...) custom-call(f32[256,1024]{1,0:T(8,128)} %emb_hbm.1, s32[2,128]{1,0:T(2,128)} %bitcast.14, ...), custom_call_target="tpu_custom_call" | custom-call | tf_op jit(solution)/shard_map/pallas_call | solution.py:749
  41.3 0.0 copy-done
  41.3 0.0 copy-done.1
  41.4 2.8 %shard_map.77 = (f32[512,1024]{1,0:T(8,128)}, s32[4,128]{1,0:T(4,128)}, s32[16,128]{1,0:T(8,128)}) custom-call(f32[512,1024]{1,0:T(8,128)S(1)} %get-tuple-element.42.rows, bf16[128,1024]{1,0:T(8,128)(2,1)S(1)} %get-tuple-element.43.hi, bf16[128,1024]{1,0:T(8,128)(2,1)} %get-tuple-element.44.lo, bf16[512,128]{1,0:T(8,128)(2,1)S(1)} %get-tuple-element.45.place, ...), custom_call_target="tpu_custom_call" | custom-call | tf_op jit(solution)/shard_map/pallas_call | solution.py:715
  (1 shorter events, 0.0 us)
Async XLA Ops:
  0.6 40.7 %copy-start = (f32[256,1024]{1,0:T(8,128)S(1)}, f32[256,1024]{1,0:T(8,128)}, u32[]{:S(2)}) copy-start(f32[256,1024]{1,0:T(8,128)} %emb_hbm.1) | copy-start | bytes 3145732
  0.6 40.7 %copy-start.1 = (s32[256]{0:T(256)S(1)}, s32[256]{0:T(256)}, u32[]{:S(2)}) copy-start(s32[256]{0:T(256)} %param.8) | copy-start | bytes 3076

commit v3 on v2

--- a/solution.py
+++ b/solution.py
@@ -245,7 +245,7 @@
             pltpu.SemaphoreType.DMA((2,)),
         ],
         compiler_params=pltpu.CompilerParams(
-            collective_id=1, has_side_effects=True, vmem_limit_bytes=48 * 1024 * 1024
+            collective_id=1, has_side_effects=True, vmem_limit_bytes=36 * 1024 * 1024
         ),
     )(send, meta, centroids, rotation)
     return packed
@@ -264,11 +264,11 @@
 
 
 def relayed_kernel(
-    n, real, near, direct, pool,
+    n, real, near, direct, pool, small,
     emb_hbm, lists_hbm, ids_hbm, cent, rot,
-    out, last_hi, last_lo, last_place, ids_out, off_out, most_out,
-    emb, lists, ids, turned_hi, turned_lo, send_a, send_b, send_x, far_out, near_out, next_out, meta, recv, far_in, near_in, next_in, meta_in,
-    part_1, part_2, part_3, cent_buf, rot_buf, rot_hi, rot_lo, res, left_hi, left_lo, place,
+    out, last, last_place, ids_out, off_out, most_out, emb_out,
+    emb, lists, ids, turned_hi, turned_lo, send_a, send_b, send_x, far_out, near_out, meta, recv, far_in, near_in, meta_in,
+    part_1, part_2, part_3, cent_buf, rot_buf, rot_hi, rot_lo, res, left, place,
     send_sem, recv_sem, load_sem,
 ):
     me = lax.axis_index("dev")
@@ -282,20 +282,20 @@
     members = n // LEVELS
     late = direct - near
     extra = real - direct
-    block = far_in.shape[0]
+    soon = (near + 1) // 2
+    block, block_near = far_in.shape[0], near_in.shape[0]
     level = lax.div(me, members)
     inside = lax.rem(me, members)
     beside = level + 1 - 2 * lax.rem(level, 2)
     across = lax.rem(level + 2, LEVELS)
     corner = lax.rem(beside + 2, LEVELS)
-    META, A, B, X, FAR, NEAR, NEXT = range(7)
+    META, A, B, X, FAR, NEAR = range(6)
 
     def flat(ref):
         return ref.reshape(ref.shape[0] * ref.shape[1] * tall, LANES) if len(ref.shape) == 4 else ref.reshape(ref.shape[0] * tall, LANES)
 
     recv_f, send_a_f, send_b_f, send_x_f = flat(recv), flat(send_a), flat(send_b), flat(send_x)
-    far_out_f, near_out_f, next_out_f = flat(far_out), flat(near_out), flat(next_out)
-    far_in_f, near_in_f, next_in_f = flat(far_in), flat(near_in), flat(next_in)
+    far_out_f, near_out_f, far_in_f, near_in_f = flat(far_out), flat(near_out), flat(far_in), flat(near_in)
     part_1_f, part_2_f, part_3_f = flat(part_1), flat(part_2), flat(part_3)
 
     def tile_of(index):
@@ -348,49 +348,47 @@
     seat = lax.broadcasted_iota(jnp.int32, (8, LANES), 0)
     triangle = hot(ahead)
     done = jnp.zeros((8, 1), F32)
-    side_at, gone_at, turn_at = [], [], []
+    side_at, gone_at = [], []
     for r in range(parts):
-        mask = ((seat == 0) & side[r]) | ((seat == 1) & gone[r]) | ((seat == 2) & turn[r])
+        mask = ((seat == 0) & side[r]) | ((seat == 1) & gone[r])
         flags = mask.astype(F32)
         index = (dot(flags.astype(BF16), triangle) + done).astype(jnp.int32)
         done = done + jnp.sum(flags, axis=1, keepdims=True)
         side_at.append(jnp.where(side[r], index[0:1], -1))
         gone_at.append(jnp.where(gone[r], index[1:2], -1))
-        turn_at.append(jnp.where(turn[r], index[2:3], -1))
-    worst = jnp.max(done, axis=0, keepdims=True).astype(jnp.int32)
-
-    table = lax.broadcasted_iota(jnp.int32, (2 * block, LANES), 0)
+    worst = jnp.maximum(done[0:1] + (pool - small), done[1:2]).astype(jnp.int32)
+
+    table = lax.broadcasted_iota(jnp.int32, (block + block_near, LANES), 0)
     picks = []
     for r in range(parts):
         target = jnp.where((gone_at[r] >= 0) & (gone_at[r] < pool), gone_at[r], -1)
-        target = jnp.where((side_at[r] >= 0) & (side_at[r] < pool), block + side_at[r], target)
+        target = jnp.where((side_at[r] >= 0) & (side_at[r] < small), block + side_at[r], target)
         picks.append(hot(table == target))
     pick = jnp.concatenate(picks, axis=1)
     for b in range(0, tall, 2):
         hi, lo = split(emb[:, b * LANES:(b + 2) * LANES])
-        left_hi[pl.ds(0, count), pl.ds(b * LANES, 2 * LANES)] = hi
-        left_lo[pl.ds(0, count), pl.ds(b * LANES, 2 * LANES)] = lo
+        left[pl.ds(0, count), pl.ds(b * LANES, 2 * LANES)] = hi
+        left[pl.ds(count, count), pl.ds(b * LANES, 2 * LANES)] = lo
         value = dot(pick, hi) + dot(pick, lo)
         for h in range(2):
             got = value[:, h * LANES:(h + 1) * LANES]
             far_out_f[pl.ds(b + h, block, stride=tall), :] = got[:block]
-            near_out_f[pl.ds(b + h, block, stride=tall), :] = got[block:]
+            near_out_f[pl.ds(b + h, block_near, stride=tall), :] = got[block:]
 
     far_codes = jnp.zeros((8, LANES), F32)
     near_codes = jnp.zeros((8, LANES), F32)
     for r in range(parts):
         spot = (slot_of[r] - direct) * members + lax.rem(owner_of[r], members) + 1
-        stay = gone[r] & (level_of[r] == across)
-        first = jnp.where((seat == 0) & stay, spot, 0) + jnp.where((seat == 1) & turn[r], turn_at[r] + 1, 0)
-        last = jnp.where(seat == 2, spot, 0)
-        far_codes = far_codes + dot_t(first.astype(F32).astype(BF16), hot(subs == gone_at[r]))
-        far_codes = far_codes + dot_t(last.astype(F32).astype(BF16), hot(subs == turn_at[r]))
-        near_codes = near_codes + dot_t(last.astype(F32).astype(BF16), hot(subs == side_at[r]))
+        beyond = spot + jnp.where(turn[r], extra * members, 0)
+        far_row = jnp.broadcast_to(beyond, (8, LANES)).astype(F32).astype(BF16)
+        near_row = jnp.broadcast_to(spot, (8, LANES)).astype(F32).astype(BF16)
+        far_codes = far_codes + dot_t(far_row, hot(subs == gone_at[r]))
+        near_codes = near_codes + dot_t(near_row, hot(subs == side_at[r]))
     far_out[pool] = far_codes - 1.0
-    near_out[pool] = near_codes - 1.0
+    near_out[small] = near_codes - 1.0
     blank = jnp.zeros((8, LANES), F32)
-    for ref in (far_in, near_in, next_in):
-        for k in range(pool + 1, block):
+    for ref, used in ((far_in, pool + 1), (near_in, small + 1)):
+        for k in range(used, ref.shape[0]):
             ref[k] = blank
 
     owners = lax.broadcasted_iota(jnp.int32, (n, LANES), 0)
@@ -420,29 +418,48 @@
     def settle(ref, sem):
         pltpu.make_async_copy(ref, ref, sem).wait()
 
-    def peer_of(k):
-        peer, bit = 0, 1
-        while bit < n:
-            ours = lax.rem(lax.div(me, bit), 2)
-            step = lax.rem(lax.div(k, bit), 2)
-            peer = peer + bit * lax.rem(ours + step, 2)
-            bit *= 2
-        return peer
-
-    def send_meta(k, carry):
-        peer = peer_of(k)
+    def flips(bits):
+        steps = []
+        for bit in bits:
+            steps.append(bit - 2 * bit * lax.rem(lax.div(me, bit), 2))
+        return steps
+
+    low_bits = [1, 2, 4]
+    high_bits = [8 << k for k in range((n // 8).bit_length() - 1)]
+    low_steps, high_steps = flips(low_bits), flips(high_bits)
+
+    def to_peers(send):
+        def eight(base, first):
+            for k in range(first, 8):
+                peer = base
+                for bit, step in zip(low_bits, low_steps):
+                    if k & bit:
+                        peer = peer + step
+                send(peer)
+
+        def block_of(c, carry):
+            base = me
+            for k, step in enumerate(high_steps):
+                base = base + step * lax.rem(lax.div(c, 1 << k), 2)
+            eight(base, 0)
+            return carry
+
+        eight(me, 1)
+        lax.fori_loop(1, n // 8, block_of, 0)
+
+    def send_meta(peer):
         post(meta.at[peer], meta_in.at[me], peer, META)
-        return carry
-
-    def send_first(k, carry):
-        peer = peer_of(k)
+
+    def send_first(peer):
         post(send_a.at[:, peer], recv.at[pl.ds(near, late), me], peer, A)
-        return carry
-
-    def send_second(k, carry):
-        peer = peer_of(k)
-        post(send_b.at[:, peer], recv.at[pl.ds(0, near), me], peer, B)
-        return carry
+
+    def send_second(first, size):
+        lines = pl.ds(first, size)
+
+        def send(peer):
+            post(send_b.at[lines, peer], recv.at[lines, me], peer, B)
+
+        return send
 
     def spread(ref, source):
         def one(k, carry):
@@ -451,14 +468,14 @@
             return carry
         lax.fori_loop(1, members, one, 0)
 
-    message = pl.ds(0, pool + 1)
+    far_message, near_message = pl.ds(0, pool + 1), pl.ds(0, small + 1)
     beside_dev = beside * members + inside
     across_dev = across * members + inside
     corner_dev = corner * members + inside
 
-    lax.fori_loop(1, n, send_meta, 0)
-    post(far_out.at[message], far_in.at[message], across_dev, FAR)
-    post(near_out.at[message], near_in.at[message], beside_dev, NEAR)
+    post(far_out.at[far_message], far_in.at[far_message], across_dev, FAR)
+    post(near_out.at[near_message], near_in.at[near_message], beside_dev, NEAR)
+    to_peers(send_meta)
     load_rot.wait()
     load_cent.start()
 
@@ -471,19 +488,20 @@
 
     lax.fori_loop(0, width // LANES, halve, 0)
 
-    def turn_rows(lines):
+    def turn_rows(rows):
+        both, top = pl.ds(0, 2 * rows), pl.ds(0, rows)
+
         def turned(t, carry):
             at = pl.ds(pl.multiple_of(t * 256, 256), 256)
-            r_hi = rot_hi[:, at]
-            value = dot(left_hi[lines, :], r_hi) + dot(left_lo[lines, :], r_hi) + dot(left_hi[lines, :], rot_lo[:, at])
-            hi, lo = split(value)
-            turned_hi[lines, at] = hi
-            turned_lo[lines, at] = lo
+            value = dot(left[both, :], rot_hi[:, at])
+            hi, lo = split(value[:rows] + value[rows:] + dot(left[top, :], rot_lo[:, at]))
+            turned_hi[top, at] = hi
+            turned_lo[top, at] = lo
             return carry
 
         lax.fori_loop(0, width // 256, turned, 0)
 
-    turn_rows(pl.ds(0, count))
+    turn_rows(count)
     base_x = late * n
     base_b = base_x + extra * members
     wanted = base_b + near * n
@@ -505,8 +523,9 @@
             send_a_f[pl.ds(b + h, late * n, stride=tall), :] = got[:base_x]
             send_x_f[pl.ds(b + h, extra * members, stride=tall), :] = got[base_x:base_b]
             send_b_f[pl.ds(b + h, near * n, stride=tall), :] = got[base_b:]
-    lax.fori_loop(1, n, send_first, 0)
+    to_peers(send_first)
     spread(send_x, me)
+    to_peers(send_second(0, soon))
     for s in range(late):
         recv_f[tile_of((near + s) * n + me), :] = send_a_f[tile_of(s * n + me), :]
     for s in range(near):
@@ -514,6 +533,8 @@
     for s in range(extra):
         recv_f[tile_of((direct + s) * n + me), :] = send_x_f[tile_of(s * members + inside), :]
 
+    keep_emb = pltpu.make_async_copy(emb, emb_out, load_sem.at[5])
+    keep_emb.start()
     span_meta = meta_in.at[pl.ds(0, n - 1)]
     settle(span_meta, recv_sem.at[META])
 
@@ -565,52 +586,46 @@
     def pair(ref, first, rows, b):
         return split(jnp.concatenate([piece(ref, first, rows, b), piece(ref, first, rows, b + 1)], axis=1))
 
-    seats = lax.broadcasted_iota(jnp.int32, (extra * members, block), 0)
-
-    def expand(codes, source, target, forward, raw):
-        choose = hot(seats == codes[0][:, :block].astype(jnp.int32))
-        if forward is not None:
-            onward = lax.broadcasted_iota(jnp.int32, (block, block), 0) == codes[1][:, :block].astype(jnp.int32)
-            choose = jnp.concatenate([choose, hot(onward)], axis=0)
-        lines = pl.ds(0, block)
-        if raw:
-            for b in range(0, tall, 2):
-                cols = pl.ds(b * LANES, 2 * LANES)
-                hi, lo = pair(source, 0, block, b)
-                left_hi[lines, cols] = hi
-                left_lo[lines, cols] = lo
-            turn_rows(lines)
+    def expand(source, rows, used, targets):
+        high = len(targets) * extra * members
+        code = source[pl.ds(used * tall, 1), :][:, :rows].astype(jnp.int32)
+        choose = hot(lax.broadcasted_iota(jnp.int32, (high, rows), 0) == code)
         for b in range(0, tall, 2):
-            if raw:
-                cols = pl.ds(b * LANES, 2 * LANES)
-                hi, lo = turned_hi[lines, cols], turned_lo[lines, cols]
-            else:
-                hi, lo = pair(source, 0, block, b)
-            value = dot(choose, hi) + dot(choose, lo)
-            for h in range(2):
-                part = value[:, h * LANES:(h + 1) * LANES]
-                target[pl.ds(b + h, extra * members, stride=tall), :] = part[:extra * members]
-                if forward is not None:
-                    forward[pl.ds(b + h, block, stride=tall), :] = part[extra * members:]
+            cols = pl.ds(b * LANES, 2 * LANES)
+            hi, lo = pair(source, 0, rows, b)
+            left[pl.ds(0, rows), cols] = hi
+            left[pl.ds(rows, rows), cols] = lo
+        turn_rows(rows)
+        for b in range(0, tall, 2):
+            cols = pl.ds(b * LANES, 2 * LANES)
+            value = dot(choose, turned_hi[pl.ds(0, rows), cols]) + dot(choose, turned_lo[pl.ds(0, rows), cols])
+            for k, target in enumerate(targets):
+                for h in range(2):
+                    part = value[k * extra * members:(k + 1) * extra * members, h * LANES:(h + 1) * LANES]
+                    target[pl.ds(b + h, extra * members, stride=tall), :] = part
 
     def keep(ref, source):
         for s in range(extra):
             recv_f[tile_of((direct + s) * n + source), :] = ref[tile_of(s * members + inside), :]
 
-    settle(near_in.at[message], recv_sem.at[NEAR])
-    expand([near_in[pool][2:3]], near_in_f, part_1_f, None, True)
+    settle(near_in.at[near_message], recv_sem.at[NEAR])
+    expand(near_in_f, block_near, small, [part_1_f])
     spread(part_1, beside_dev)
     keep(part_1_f, beside_dev)
 
-    settle(far_in.at[message], recv_sem.at[FAR])
-    codes = far_in[pool]
-    expand([codes[0:1], codes[1:2]], far_in_f, part_2_f, next_out_f, True)
-    next_out[pool] = codes
-    post(next_out.at[message], next_in.at[message], beside_dev, NEXT)
+    settle(far_in.at[far_message], recv_sem.at[FAR])
+    expand(far_in_f, block, pool, [part_2_f, part_3_f])
+
+    def send_over(k, carry):
+        other = lax.rem(inside + k, members)
+        post(part_3.at[:, other], recv.at[pl.ds(direct, extra), across_dev], beside * members + other, X)
+        return carry
+
+    lax.fori_loop(0, members, send_over, 0)
     spread(part_2, across_dev)
     keep(part_2_f, across_dev)
-
-    lax.fori_loop(1, n, send_second, 0)
+    if near > soon:
+        to_peers(send_second(soon, near - soon))
 
     for q in range(cap // LANES):
         total = jnp.zeros((1, LANES), jnp.int32)
@@ -641,28 +656,24 @@
 
     lax.fori_loop(0, owned // step, centre, 0)
 
-    settle(next_in.at[message], recv_sem.at[NEXT])
-    expand([next_in[pool][2:3]], next_in_f, part_3_f, None, False)
-    spread(part_3, corner_dev)
-    keep(part_3_f, corner_dev)
-
     for b in range(0, tall, 2):
         cols = pl.ds(b * LANES, 2 * LANES)
         hi, lo = split(res[:, cols])
-        left_hi[:, cols] = hi
-        left_lo[:, cols] = lo
+        left[pl.ds(0, cap), cols] = hi
+        left[pl.ds(cap, cap), cols] = lo
 
     def tile(t, carry):
         at = pl.ds(pl.multiple_of(t * 256, 256), 256)
         r_hi = rot_hi[:, at]
-        out[:, at] = dot(left_hi[...], r_hi) + dot(left_lo[...], r_hi) + dot(left_hi[...], rot_lo[:, at])
+        top, low = left[pl.ds(0, cap), :], left[pl.ds(cap, cap), :]
+        out[:, at] = dot(top, r_hi) + dot(low, r_hi) + dot(top, rot_lo[:, at])
         return carry
 
     lax.fori_loop(0, width // 256, tile, 0)
 
     span_a = recv.at[pl.ds(near, late), pl.ds(0, n - 1)]
     settle(span_a, recv_sem.at[A])
-    span_x = recv_f.at[pl.ds(0, LEVELS * extra * (members - 1) * tall)]
+    span_x = recv_f.at[pl.ds(0, extra * (LEVELS * members - LEVELS + 1) * tall)]
     settle(span_x, recv_sem.at[X])
     rest = entries - near * n
     for b in range(0, tall, 2):
@@ -672,24 +683,25 @@
         out[:, cols] += dot(spots, hi) + dot(spots, lo)
 
     span_b = recv.at[pl.ds(0, near), pl.ds(0, n - 1)]
+    last_place[:, :near * n] = place[:, :near * n]
+    last_place[:, near * n:] = place[:, :near * n]
     settle(span_b, recv_sem.at[B])
     for b in range(0, tall, 2):
         cols = pl.ds(b * LANES, 2 * LANES)
         hi, lo = pair(recv_f, 0, near * n, b)
-        last_hi[:, cols] = hi
-        last_lo[:, cols] = lo
-    last_place[...] = place[:, :near * n]
-
+        last[pl.ds(0, near * n), cols] = hi
+        last[pl.ds(near * n, near * n), cols] = lo
+
+    keep_emb.wait()
     settle(span_meta, send_sem.at[META])
     settle(span_a, send_sem.at[A])
     settle(span_b, send_sem.at[B])
     settle(span_x, send_sem.at[X])
-    settle(far_in.at[message], send_sem.at[FAR])
-    settle(near_in.at[message], send_sem.at[NEAR])
-    settle(next_in.at[message], send_sem.at[NEXT])
-
-
-def finish_kernel(rows, hi, lo, place, ids, offsets, rows_out, ids_out, off_out, buf, sem):
+    settle(far_in.at[far_message], send_sem.at[FAR])
+    settle(near_in.at[near_message], send_sem.at[NEAR])
+
+
+def finish_kernel(pool, most, rows, last, place, ids, offsets, rows_out, ids_out, off_out, buf, sem):
     wide = 256
     tiles = rows.shape[1] // wide
     moves = [
@@ -700,7 +712,8 @@
         move.start()
     for t in range(tiles):
         cols = pl.ds(t * wide, wide)
-        buf[t] = rows[:, cols] + dot(place[...], hi[:, cols]) + dot(place[...], lo[:, cols])
+        kept = rows[:, cols]
+        buf[t] = jnp.where(most[0:1, 0:1] > pool, kept, kept + dot(place[...], last[:, cols]))
         move = pltpu.make_async_copy(buf.at[t], rows_out.at[:, cols], sem.at[t])
         move.start()
         moves.append(move)
@@ -708,22 +721,23 @@
         move.wait()
 
 
-def finish(rows, hi, lo, place, ids, offsets):
+def finish(pool, most, rows, last, place, ids, offsets):
     vmem = pl.BlockSpec(memory_space=pltpu.VMEM)
     hbm = pl.BlockSpec(memory_space=pltpu.HBM)
     cap, width = rows.shape
     return pl.pallas_call(
-        finish_kernel,
+        functools.partial(finish_kernel, pool),
         out_shape=tuple(jax.ShapeDtypeStruct(x.shape, x.dtype) for x in (rows, ids, offsets)),
         in_specs=[vmem] * 6,
         out_specs=(hbm,) * 3,
         scratch_shapes=[pltpu.VMEM((width // 256, cap, 256), F32), pltpu.SemaphoreType.DMA((width // 256 + 2,))],
-        compiler_params=pltpu.CompilerParams(vmem_limit_bytes=16 * 1024 * 1024),
-    )(rows, hi, lo, place, ids, offsets)
+        compiler_params=pltpu.CompilerParams(vmem_limit_bytes=8 * 1024 * 1024),
+    )(most, rows, last, place, ids, offsets)
 
 
 LEVELS = 4
-POOL = 46
+POOL = 44
+SMALL = 34
 
 
 def local(embeddings, lists, row_ids, centroids, rotation):
@@ -736,8 +750,8 @@
     direct = (7 * real + 8) // 16
     late, extra = direct - near, real - direct
     members = n // LEVELS
-    pool = POOL
-    block = -(-(pool + 1) // 16) * 16
+    pool, small = POOL, SMALL
+    block, block_near = -(-(pool + 1) // 16) * 16, -(-(small + 1) // 16) * 16
     tall = width // LANES
     by_lane = (row_count // LANES, LANES)
     vmem = pl.BlockSpec(memory_space=pltpu.VMEM)
@@ -746,28 +760,28 @@
     def rows_of(*lead):
         return pltpu.VMEM((*lead, tall, LANES), F32)
 
-    packed, hi, lo, place, ids, offsets, most = pl.pallas_call(
-        functools.partial(relayed_kernel, n, real, near, direct, pool),
+    packed, last, place, ids, offsets, most, copied = pl.pallas_call(
+        functools.partial(relayed_kernel, n, real, near, direct, pool, small),
         out_shape=(
             jax.ShapeDtypeStruct((cap, width), F32),
-            jax.ShapeDtypeStruct((near * n, width), BF16),
-            jax.ShapeDtypeStruct((near * n, width), BF16),
-            jax.ShapeDtypeStruct((cap, near * n), BF16),
+            jax.ShapeDtypeStruct((2 * near * n, width), BF16),
+            jax.ShapeDtypeStruct((cap, 2 * near * n), BF16),
             jax.ShapeDtypeStruct((cap // LANES, LANES), jnp.int32),
             jax.ShapeDtypeStruct((owned // LANES, LANES), jnp.int32),
             jax.ShapeDtypeStruct((1, LANES), jnp.int32),
+            jax.ShapeDtypeStruct((row_count, width), F32),
         ),
         in_specs=[hbm] * 5,
-        out_specs=(vmem,) * 7,
+        out_specs=(vmem,) * 6 + (hbm,),
         scratch_shapes=[
             pltpu.VMEM((row_count, width), F32),
             pltpu.VMEM(by_lane, jnp.int32),
             pltpu.VMEM(by_lane, jnp.int32),
             pltpu.VMEM((row_count, width), BF16),
             pltpu.VMEM((row_count, width), BF16),
-            rows_of(late, n), rows_of(near, n), rows_of(extra, members), rows_of(block), rows_of(block), rows_of(block),
+            rows_of(late, n), rows_of(near, n), rows_of(extra, members), rows_of(block), rows_of(block_near),
             pltpu.VMEM((n, 1, LANES), jnp.int32),
-            rows_of(real, n), rows_of(block), rows_of(block), rows_of(block),
+            rows_of(real, n), rows_of(block), rows_of(block_near),
             pltpu.VMEM((n, 1, LANES), jnp.int32),
             rows_of(extra, members), rows_of(extra, members), rows_of(extra, members),
             pltpu.VMEM((owned, width), F32),
@@ -775,23 +789,22 @@
             pltpu.VMEM((width, width), BF16),
             pltpu.VMEM((width, width), BF16),
             pltpu.VMEM((cap, width), F32),
-            pltpu.VMEM((cap, width), BF16),
-            pltpu.VMEM((cap, width), BF16),
+            pltpu.VMEM((2 * cap, width), BF16),
             pltpu.VMEM((cap, n * real), BF16),
-            pltpu.SemaphoreType.DMA((7,)),
-            pltpu.SemaphoreType.DMA((7,)),
-            pltpu.SemaphoreType.DMA((5,)),
+            pltpu.SemaphoreType.DMA((6,)),
+            pltpu.SemaphoreType.DMA((6,)),
+            pltpu.SemaphoreType.DMA((6,)),
         ],
         compiler_params=pltpu.CompilerParams(
-            collective_id=0, has_side_effects=True, vmem_limit_bytes=48 * 1024 * 1024
+            collective_id=0, has_side_effects=True, vmem_limit_bytes=36 * 1024 * 1024
         ),
     )(embeddings, lists.reshape(by_lane), row_ids.reshape(by_lane), centroids, rotation)
-    packed, hi, lo = lax.cond(
+    packed = lax.cond(
         most[0, 0] > pool,
-        lambda: (full(embeddings, lists, row_ids, centroids, rotation), jnp.zeros_like(hi), jnp.zeros_like(lo)),
-        lambda: (packed, hi, lo),
+        lambda: full(copied, lists, row_ids, centroids, rotation),
+        lambda: packed,
     )
-    packed, ids, offsets = finish(packed, hi, lo, place, ids, offsets)
+    packed, ids, offsets = finish(pool, most, packed, last, place, ids, offsets)
     return packed, ids.reshape(-1), offsets.reshape(-1)
 
 

time: 44.3 us -> 41.8 us (0.944)
  Pallas kernels: 43.4 us -> 39.7 us
  local copies, waits for them, and re-layouts: 0.01 us -> 1.23 us
    pallas_call x1, Pallas kernels: 40.6 us -> 38 us  [local(): pl.pallas_call(functools.partial(relayed_kernel, n, real, near, direct, p...]
    unnamed x4 -> x6, local copies, waits for them, and re-layouts: 0.01 us -> 1.23 us
    pallas_call x1, Pallas kernels: 2.76 us -> 1.68 us  [finish(): pl.pallas_call(functools.partial(finish_kernel, pool), out_shape=tuple((j...]
where the time goes in v3:
time: 41.8 us; the launch traced here: 41.6 us
  Pallas kernels  39.7 us (95%)
  local copies, waits for them, and re-layouts  1.23 us (3%)
  between operations  0.71 us (2%)
    pallas_call x1, Pallas kernels, local(): pl.pallas_call(functools.partial(relayed_kernel, n, real, near, direct, p...  38 us
    pallas_call x1, Pallas kernels, finish(): pl.pallas_call(functools.partial(finish_kernel, pool), out_shape=tuple((j...  1.68 us
    unnamed x6, local copies, waits for them, and re-layouts  1.23 us

profile of v3, /device:TPU:0, one launch (start us, length us, event | category | flops | bytes accessed | tf_op | source)
XLA Modules:
  0.0 41.6 jit_solution(1910349683456559553)
XLA Ops:
  0.6 0.0 copy-start
  0.6 1.2 %copy-done = f32[256,1024]{1,0:T(8,128)S(1)} copy-done((f32[256,1024]{1,0:T(8,128)S(1)}, f32[256,1024]{1,0:T(8,128)}, u32[]{:S(2)}) %copy-start) | copy-done | bytes 1048600
  1.9 0.0 copy-start.1
  1.9 0.0 copy-start.2
  1.9 38.0 %shard_map.76 = (f32[512,1024]{1,0:T(8,128)S(1)}, bf16[256,1024]{1,0:T(8,128)(2,1)S(1)}, bf16[512,256]{1,0:T(8,128)(2,1)S(1)}, s32[4,128]{1,0:T(4,128)S(1)}, s32...) custom-call(f32[256,1024]{1,0:T(8,128)S(1)} %copy-done, s32[2,128]{1,0:T(2,128)} %bitcast.14, ...), custom_call_target="tpu_custom_call" | custom-call | tf_op jit(solution)/shard_map/pallas_call | solution.py:763
  39.9 0.0 copy-done.1
  39.9 0.0 copy-done.2
  39.9 1.7 %shard_map.77 = (f32[512,1024]{1,0:T(8,128)}, s32[4,128]{1,0:T(4,128)}, s32[16,128]{1,0:T(8,128)}) custom-call(s32[1,128]{1,0:T(1,128)S(1)} %get-tuple-element.33.most, f32[512,1024]{1,0:T(8,128)S(1)} %get-tuple-element.49.rows, bf16[256,1024]{1,0:T(8,128)(2,1)S(1)} %get-tuple-element.36.last, bf16[512,256]{1,0:T(8,128)(2,1)S(1)} %get-tuple-element.37.place, ...), custom_call_target="tpu_custom_call" | custom-call | tf_op jit(solution)/shard_map/pallas_call | solution.py:728
  (1 shorter events, 0.0 us)
Async XLA Ops:
  0.6 1.2 %copy-start = (f32[256,1024]{1,0:T(8,128)S(1)}, f32[256,1024]{1,0:T(8,128)}, u32[]{:S(2)}) copy-start(f32[256,1024]{1,0:T(8,128)} %emb_hbm.1) | copy-start | bytes 3145732
  1.9 38.0 %copy-start.1 = (s32[256]{0:T(256)S(1)}, s32[256]{0:T(256)}, u32[]{:S(2)}) copy-start(s32[256]{0:T(256)} %param.8) | copy-start | bytes 3076
  1.9 38.1 %copy-start.2 = (s32[256]{0:T(256)S(1)}, s32[256]{0:T(256)}, u32[]{:S(2)}) copy-start(s32[256]{0:T(256)} %param.9) | copy-start | bytes 3076

commit v4 on v3

--- a/solution.py
+++ b/solution.py
@@ -268,7 +268,7 @@
     emb_hbm, lists_hbm, ids_hbm, cent, rot,
     out, last, last_place, ids_out, off_out, most_out, emb_out,
     emb, lists, ids, turned_hi, turned_lo, send_a, send_b, send_x, far_out, near_out, meta, recv, far_in, near_in, meta_in,
-    part_1, part_2, part_3, cent_buf, rot_buf, rot_hi, rot_lo, res, left, place,
+    part_1, part_2, part_3, cent_buf, rot_buf, rot_hi, rot_lo, res, left, place, place_twice,
     send_sem, recv_sem, load_sem,
 ):
     me = lax.axis_index("dev")
@@ -671,16 +671,17 @@
 
     lax.fori_loop(0, width // 256, tile, 0)
 
+    rest = entries - near * n
+    place_twice[:, :rest] = place[:, near * n:]
+    place_twice[:, rest:] = place[:, near * n:]
     span_a = recv.at[pl.ds(near, late), pl.ds(0, n - 1)]
     settle(span_a, recv_sem.at[A])
     span_x = recv_f.at[pl.ds(0, extra * (LEVELS * members - LEVELS + 1) * tall)]
     settle(span_x, recv_sem.at[X])
-    rest = entries - near * n
     for b in range(0, tall, 2):
         cols = pl.ds(b * LANES, 2 * LANES)
         hi, lo = pair(recv_f, near * n, rest, b)
-        spots = place[:, near * n:]
-        out[:, cols] += dot(spots, hi) + dot(spots, lo)
+        out[:, cols] += dot(place_twice[...], jnp.concatenate([hi, lo], axis=0))
 
     span_b = recv.at[pl.ds(0, near), pl.ds(0, n - 1)]
     last_place[:, :near * n] = place[:, :near * n]
@@ -791,12 +792,13 @@
             pltpu.VMEM((cap, width), F32),
             pltpu.VMEM((2 * cap, width), BF16),
             pltpu.VMEM((cap, n * real), BF16),
+            pltpu.VMEM((cap, 2 * (n * real - near * n)), BF16),
             pltpu.SemaphoreType.DMA((6,)),
             pltpu.SemaphoreType.DMA((6,)),
             pltpu.SemaphoreType.DMA((6,)),
         ],
         compiler_params=pltpu.CompilerParams(
-            collective_id=0, has_side_effects=True, vmem_limit_bytes=36 * 1024 * 1024
+            collective_id=0, has_side_effects=True, vmem_limit_bytes=55200000
         ),
     )(embeddings, lists.reshape(by_lane), row_ids.reshape(by_lane), centroids, rotation)
     packed = lax.cond(

time: 41.8 us -> 41.2 us (0.986)
  local copies, waits for them, and re-layouts: 1.23 us -> 0.01 us
  Pallas kernels: 39.7 us -> 40.3 us
    unnamed x6 -> x4, local copies, waits for them, and re-layouts: 1.23 us -> 0.01 us
    pallas_call x1, Pallas kernels: 38 us -> 38.7 us  [local(): pl.pallas_call(functools.partial(relayed_kernel, n, real, near, direct, p...]
where the time goes in v4:
time: 41.2 us; the launch traced here: 41.1 us
  Pallas kernels  40.3 us (98%)
  between operations  0.71 us (2%)
    pallas_call x1, Pallas kernels, local(): pl.pallas_call(functools.partial(relayed_kernel, n, real, near, direct, p...  38.7 us
    pallas_call x1, Pallas kernels, finish(): pl.pallas_call(functools.partial(finish_kernel, pool), out_shape=tuple((j...  1.68 us

profile of v4, /device:TPU:0, one launch (start us, length us, event | category | flops | bytes accessed | tf_op | source)
XLA Modules:
  0.0 41.1 jit_solution(8779770227188366720)
XLA Ops:
  0.6 0.0 copy-start
  0.6 0.0 copy-start.1
  0.7 38.7 %shard_map.76 = (f32[512,1024]{1,0:T(8,128)S(1)}, bf16[256,1024]{1,0:T(8,128)(2,1)S(1)}, bf16[512,256]{1,0:T(8,128)(2,1)S(1)}, s32[4,128]{1,0:T(4,128)S(1)}, s32...) custom-call(f32[256,1024]{1,0:T(8,128)} %emb_hbm.1, s32[2,128]{1,0:T(2,128)} %bitcast.14, ...), custom_call_target="tpu_custom_call" | custom-call | tf_op jit(solution)/shard_map/pallas_call | solution.py:764
  39.4 0.0 copy-done
  39.4 0.0 copy-done.1
  39.4 1.7 %shard_map.77 = (f32[512,1024]{1,0:T(8,128)}, s32[4,128]{1,0:T(4,128)}, s32[16,128]{1,0:T(8,128)}) custom-call(s32[1,128]{1,0:T(1,128)S(1)} %get-tuple-element.33.most, f32[512,1024]{1,0:T(8,128)S(1)} %get-tuple-element.49.rows, bf16[256,1024]{1,0:T(8,128)(2,1)S(1)} %get-tuple-element.36.last, bf16[512,256]{1,0:T(8,128)(2,1)S(1)} %get-tuple-element.37.place, ...), custom_call_target="tpu_custom_call" | custom-call | tf_op jit(solution)/shard_map/pallas_call | solution.py:729
  (1 shorter events, 0.0 us)
Async XLA Ops:
  0.6 38.7 %copy-start = (s32[256]{0:T(256)S(1)}, s32[256]{0:T(256)}, u32[]{:S(2)}) copy-start(s32[256]{0:T(256)} %param.8) | copy-start | bytes 3076
  0.6 38.7 %copy-start.1 = (s32[256]{0:T(256)S(1)}, s32[256]{0:T(256)}, u32[]{:S(2)}) copy-start(s32[256]{0:T(256)} %param.9) | copy-start | bytes 3076
